TPU v7x, 32 devices: a whole 2x2x4 slice. The times are simulated.
32 devices in a mesh: third: 4 (over z), second: 2 (over y), group: 4 (over x, core).
Axes of the slice: x: 2, y: 2, z: 4, core: 2. Of those that a mesh axis runs over, the one named last changes fastest.
Arguments:
- x_one: bfloat16 [65536, 768], P(('third', 'second', 'group'))
- z_one: bfloat16 [65536, 3072], P(('third', 'second', 'group'))
- x_two: bfloat16 [65536, 768], P(('third', 'second', 'group'))
- z_two: bfloat16 [65536, 3072], P(('third', 'second', 'group'))
- grad_out: bfloat16 [65536, 768], P(('third', 'second', 'group'))
- w1_in: bfloat16 [768, 3072], replicated
- w1_out: bfloat16 [3072, 768], replicated
- w2_in: bfloat16 [768, 3072], replicated
- w2_out: bfloat16 [3072, 768], replicated
Outputs:
- output 1: float32 [3072, 768], replicated
- output 2: float32 [768, 3072], replicated
- output 3: float32 [3072, 768], replicated
- output 4: float32 [768, 3072], replicated
- output 5: bfloat16 [65536, 768], P(('third', 'second', 'group'))
All inputs are finite; a program needn't handle non-finite values.
Results may differ from a plain program's by a relative error of at most 0.00509931.
Values are sent between devices in bfloat16 or wider.
A program may use at most 1 GiB of HBM per device.

v0:
```python
import math
import jax
import jax.numpy as jnp
from jax import lax
from jax.sharding import PartitionSpec as P

AXES = ('third', 'second', 'group')
INV_ROOT_TWO = math.sqrt(0.5)
INV_ROOT_TWO_PI = 1.0 / math.sqrt(2.0 * math.pi)
CONTRACT_ROWS = (((0,), (0,)), ((), ()))
CONTRACT_COLS = (((1,), (1,)), ((), ()))


def gelu_pair(z_pre):
    z_val = z_pre.astype(jnp.float32)
    cdf_val = 0.5 * (1.0 + lax.erf(z_val * INV_ROOT_TWO))
    hidden = (z_val * cdf_val).astype(jnp.bfloat16)
    slope = cdf_val + z_val * jnp.exp(-0.5 * z_val * z_val) * INV_ROOT_TWO_PI
    return hidden, slope


def block_backward(x_in, z_pre, grad_y, w_in, w_out):
    hidden, slope = gelu_pair(z_pre)
    w_out_grad = lax.dot_general(hidden, grad_y, CONTRACT_ROWS, preferred_element_type=jnp.float32).astype(jnp.bfloat16)
    grad_hidden = lax.dot_general(grad_y, w_out, CONTRACT_COLS, preferred_element_type=jnp.float32)
    grad_pre = (grad_hidden * slope).astype(jnp.bfloat16)
    w_in_grad = lax.dot_general(x_in, grad_pre, CONTRACT_ROWS, preferred_element_type=jnp.float32).astype(jnp.bfloat16)
    grad_x = (grad_y.astype(jnp.float32) + lax.dot_general(grad_pre, w_in, CONTRACT_COLS, preferred_element_type=jnp.float32)).astype(jnp.bfloat16)
    return w_out_grad, w_in_grad, grad_x


def reduce_grad(grad, group_size):
    row_count, col_count = grad.shape
    pieces = grad.reshape(group_size, row_count // group_size, col_count)
    received = lax.all_to_all(pieces, 'group', 0, 0)
    part_sum = jnp.sum(received, axis=0, dtype=jnp.float32)
    part_sum = lax.psum_scatter(part_sum, 'second', scatter_dimension=0, tiled=True)
    part_sum = lax.psum_scatter(part_sum, 'third', scatter_dimension=0, tiled=True)
    full_sum = lax.all_gather(part_sum, 'third', axis=0, tiled=True)
    full_sum = lax.all_gather(full_sum, 'second', axis=0, tiled=True)
    return lax.all_gather(full_sum, 'group', axis=0, tiled=True)


def solution(mesh):
    group_size = mesh.shape['group']

    def device_step(x_one, z_one, x_two, z_two, grad_out, w1_in, w1_out, w2_in, w2_out):
        w2o_grad, w2i_grad, dx_two = block_backward(x_two, z_two, grad_out, w2_in, w2_out)
        sum_w2o = reduce_grad(w2o_grad, group_size)
        sum_w2i = reduce_grad(w2i_grad, group_size)
        w1o_grad, w1i_grad, dx_one = block_backward(x_one, z_one, dx_two, w1_in, w1_out)
        sum_w1o = reduce_grad(w1o_grad, group_size)
        sum_w1i = reduce_grad(w1i_grad, group_size)
        return sum_w2o, sum_w2i, sum_w1o, sum_w1i, dx_one

    row_spec = P(AXES, None)
    repl_spec = P()
    return jax.shard_map(
        device_step,
        mesh=mesh,
        in_specs=(row_spec, row_spec, row_spec, row_spec, row_spec, repl_spec, repl_spec, repl_spec, repl_spec),
        out_specs=(repl_spec, repl_spec, repl_spec, repl_spec, row_spec),
        check_vma=False,
    )
```

profile of v0, /device:TPU:0, one launch (start us, length us, event | category | flops | bytes accessed | tf_op | source)
XLA Modules:
  0.0 1040.5 jit_solution(9790634721167424268)
XLA Ops:
  7.2 15.5 %fusion.22 = bf16[3072,768]{1,0:T(8,128)(2,1)} fusion(bf16[2048,768]{1,0:T(8,128)(2,1)} %param.13, bf16[2048,3072]{1,0:T(8,128)(2,1)} %param.12), kind=kOutput, calls=%fused_computation.36 | convolution fusion | flops 9703784448 | bytes 20447232 | tf_op jit(solution)/shard_map/dot_general | solution.py:24
  22.7 4.9 all-to-all-start
  27.7 0.0 reduce-scatter.9.cloned.1.call-start
  27.7 23.6 %fusion.8 = bf16[2048,3072]{1,0:T(8,128)(2,1)} fusion(bf16[2048,3072]{1,0:T(8,128)(2,1)} %param.12, bf16[2048,768]{1,0:T(8,128)(2,1)} %param.13, bf16[3072,768]{1,0:T(8,128)(2,1)} %param.17), kind=kOutput, calls=%fused_computation.18 | convolution fusion | flops 9732882432 | bytes 33030144 | tf_op jit(solution)/shard_map/dot_general | solution.py:25
  51.3 30.6 %all-to-all-done = bf16[4,768,768]{2,1,0:T(8,128)(2,1)} async-done(((bf16[4,768,768]{2,1,0:T(8,128)(2,1)}), bf16[4,768,768]{2,1,0:T(8,128)(2,1)}, u32[]{:S(2)}, u32[]{:S(2)}) %all-to-all-start) | async-done | bytes 4718624 | tf_op jit(solution)/shard_map/all_to_all | solution.py:35
  81.9 4.6 convert_reduce_fusion.3
  86.6 14.4 %convolution_convert_fusion.1 = bf16[3072,768]{0,1:T(8,128)(2,1)} fusion(bf16[2048,3072]{1,0:T(8,128)(2,1)} %fusion.8, bf16[2048,768]{1,0:T(8,128)(2,1)S(1)} %copy-done), kind=kOutput, calls=%fused_computation.39 | convolution fusion | flops 9666035712 | bytes 20447232 | tf_op jit(solution)/shard_map/dot_general | solution.py:27
  101.0 5.2 all-to-all-start.1
  106.2 0.2 reduce-scatter.13.cloned.1.call-start
  106.5 15.5 %add_convert_fusion.1 = bf16[2048,768]{1,0:T(8,128)(2,1)} fusion(bf16[2048,768]{1,0:T(8,128)(2,1)S(1)} %copy-done.3, bf16[2048,3072]{1,0:T(8,128)(2,1)} %fusion.8, bf16[768,3072]{1,0:T(8,128)(2,1)} %param.16), kind=kOutput, calls=%fused_computation.35 | convolution fusion | flops 9668395008 | bytes 23592960 | tf_op jit(solution)/shard_map/dot_general | solution.py:28
  121.9 37.8 %all-to-all-done.1 = bf16[4,192,3072]{2,1,0:T(8,128)(2,1)} async-done(((bf16[4,192,3072]{2,1,0:T(8,128)(2,1)}), bf16[4,192,3072]{2,1,0:T(8,128)(2,1)}, u32[]{:S(2)}, u32[]{:S(2)}) %all-to-all-start.1) | async-done | bytes 4718624 | tf_op jit(solution)/shard_map/all_to_all | solution.py:35
  159.7 4.8 convert_reduce_fusion.2
  164.6 14.5 %fusion.25 = bf16[3072,768]{1,0:T(8,128)(2,1)} fusion(bf16[2048,768]{1,0:T(8,128)(2,1)S(1)} %copy-done.5, bf16[2048,3072]{1,0:T(8,128)(2,1)} %param.10), kind=kOutput, calls=%fused_computation.37 | convolution fusion | flops 9703784448 | bytes 20447232 | tf_op jit(solution)/shard_map/dot_general | solution.py:24
  179.1 4.9 all-to-all-start.2
  184.0 0.0 reduce-scatter.17.cloned.1.call-start
  184.1 22.6 %fusion.17 = bf16[2048,3072]{1,0:T(8,128)(2,1)} fusion(bf16[2048,3072]{1,0:T(8,128)(2,1)} %param.10, bf16[2048,768]{1,0:T(8,128)(2,1)S(1)} %copy-done.5, bf16[3072,768]{1,0:T(8,128)(2,1)} %param.15), kind=kOutput, calls=%fused_computation.27 | convolution fusion | flops 9732882432 | bytes 33030144 | tf_op jit(solution)/shard_map/dot_general | solution.py:25
  206.6 30.9 %all-to-all-done.2 = bf16[4,768,768]{2,1,0:T(8,128)(2,1)} async-done(((bf16[4,768,768]{2,1,0:T(8,128)(2,1)}), bf16[4,768,768]{2,1,0:T(8,128)(2,1)}, u32[]{:S(2)}, u32[]{:S(2)}) %all-to-all-start.2) | async-done | bytes 4718624 | tf_op jit(solution)/shard_map/all_to_all | solution.py:35
  237.5 4.6 convert_reduce_fusion.1
  242.2 0.3 reduce-scatter.21.cloned.1.call-start
  242.5 13.0 %convolution_convert_fusion = bf16[3072,768]{0,1:T(8,128)(2,1)S(1)} fusion(bf16[2048,3072]{1,0:T(8,128)(2,1)} %fusion.17, bf16[2048,768]{1,0:T(8,128)(2,1)S(1)} %copy-done.4), kind=kOutput, calls=%fused_computation.38 | convolution fusion | flops 9666035712 | bytes 20447232 | tf_op jit(solution)/shard_map/dot_general | solution.py:27
  255.5 56.3 %all_to_all.20 = bf16[4,192,3072]{2,1,0:T(8,128)(2,1)S(1)} all-to-all(bf16[4,192,3072]{2,1,0:T(8,128)(2,1)S(1)} %bitcast.27), channel_id=1, replica_groups=mesh['third'=4,'second'=2,'group'=4] {'group'}, dimensions={0} | all-to-all | bytes 9437184 | tf_op jit(solution)/shard_map/all_to_all | solution.py:35
  311.9 2.3 convert_reduce_fusion
  314.2 0.0 reduce-scatter.11.cloned.1.call-start
  314.2 0.0 reduce-scatter.9.cloned.1.call-done
  314.2 0.5 reduce-scatter.11.cloned.1.call-update
  314.7 0.0 reduce-scatter.15.cloned.1.call-start
  314.8 0.5 reduce-scatter.15.cloned.1.call-update
  315.3 0.0 reduce-scatter.19.cloned.1.call-start
  315.4 0.7 reduce-scatter.19.cloned.1.call-update
  316.1 0.0 reduce-scatter.23.cloned.1.call-start
  316.1 34.0 %reduce-scatter.21.cloned.1.call-done = f32[96,3072]{1,0:T(8,128)} async-done(((f32[192,3072]{1,0:T(8,128)}), f32[96,3072]{1,0:T(8,128)}) %reduce-scatter.21.cloned.1.call-update) | async-done | bytes 1179664 | tf_op jit(solution)/shard_map/reduce_scatter | solution.py:37
  350.1 0.0 all-gather.13.cloned.1.call-start
  350.2 31.5 %reduce-scatter.11.cloned.1.call-done = f32[96,768]{1,0:T(8,128)} async-done(((f32[384,768]{1,0:T(8,128)}), f32[96,768]{1,0:T(8,128)}) %reduce-scatter.11.cloned.1.call-update) | async-done | bytes 294928 | tf_op jit(solution)/shard_map/reduce_scatter | solution.py:38
  381.7 0.0 all-gather.19.cloned.1.call-start
  381.8 30.0 %reduce-scatter.15.cloned.1.call-done = f32[24,3072]{1,0:T(8,128)} async-done(((f32[96,3072]{1,0:T(8,128)}), f32[24,3072]{1,0:T(8,128)}) %reduce-scatter.15.cloned.1.call-update) | async-done | bytes 294928 | tf_op jit(solution)/shard_map/reduce_scatter | solution.py:38
  411.8 0.0 all-gather.25.cloned.1.call-start
  411.9 30.2 %reduce-scatter.19.cloned.1.call-done = f32[96,768]{1,0:T(8,128)} async-done(((f32[384,768]{1,0:T(8,128)}), f32[96,768]{1,0:T(8,128)}) %reduce-scatter.19.cloned.1.call-update) | async-done | bytes 294928 | tf_op jit(solution)/shard_map/reduce_scatter | solution.py:38
  442.1 0.0 all-gather.31.cloned.1.call-start
  442.1 30.2 %reduce-scatter.23.cloned.1.call-done = f32[24,3072]{1,0:T(8,128)} async-done(((f32[96,3072]{1,0:T(8,128)}), f32[24,3072]{1,0:T(8,128)}) %reduce-scatter.23.cloned.1.call-update) | async-done | bytes 294928 | tf_op jit(solution)/shard_map/reduce_scatter | solution.py:38
  472.4 0.0 all-gather.15.cloned.1.call-start
  472.4 30.1 %all-gather.13.cloned.1.call-done = f32[384,768]{1,0:T(8,128)} async-done(((f32[96,768]{1,0:T(8,128)}), f32[384,768]{1,0:T(8,128)}) %all-gather.13.cloned.1.call-update) | async-done | bytes 1179664 | tf_op jit(solution)/shard_map/all_gather | solution.py:39
  502.5 0.0 all-gather.21.cloned.1.call-start
  502.6 30.7 %all-gather.19.cloned.1.call-done = f32[96,3072]{1,0:T(8,128)} async-done(((f32[24,3072]{1,0:T(8,128)}), f32[96,3072]{1,0:T(8,128)}) %all-gather.19.cloned.1.call-update) | async-done | bytes 1179664 | tf_op jit(solution)/shard_map/all_gather | solution.py:39
  533.3 0.0 all-gather.27.cloned.1.call-start
  533.4 30.9 %all-gather.25.cloned.1.call-done = f32[384,768]{1,0:T(8,128)} async-done(((f32[96,768]{1,0:T(8,128)}), f32[384,768]{1,0:T(8,128)}) %all-gather.25.cloned.1.call-update) | async-done | bytes 1179664 | tf_op jit(solution)/shard_map/all_gather | solution.py:39
  564.3 0.0 all-gather.33.cloned.1.call-start
  564.3 30.7 %all-gather.31.cloned.1.call-done = f32[96,3072]{1,0:T(8,128)} async-done(((f32[24,3072]{1,0:T(8,128)}), f32[96,3072]{1,0:T(8,128)}) %all-gather.31.cloned.1.call-update) | async-done | bytes 1179664 | tf_op jit(solution)/shard_map/all_gather | solution.py:39
  595.1 0.0 all-gather.17.cloned.1.call-start
  595.1 36.8 %all-gather.15.cloned.1.call-done = f32[768,768]{1,0:T(8,128)} async-done(((f32[384,768]{1,0:T(8,128)}), f32[768,768]{1,0:T(8,128)}) %all-gather.15.cloned.1.call-update) | async-done | bytes 2359312 | tf_op jit(solution)/shard_map/all_gather | solution.py:40
  632.0 0.0 all-gather.23.cloned.1.call-start
  632.0 37.3 %all-gather.21.cloned.1.call-done = f32[192,3072]{1,0:T(8,128)} async-done(((f32[96,3072]{1,0:T(8,128)}), f32[192,3072]{1,0:T(8,128)}) %all-gather.21.cloned.1.call-update) | async-done | bytes 2359312 | tf_op jit(solution)/shard_map/all_gather | solution.py:40
  669.3 0.0 all-gather.29.cloned.1.call-start
  669.4 37.3 %all-gather.27.cloned.1.call-done = f32[768,768]{1,0:T(8,128)} async-done(((f32[384,768]{1,0:T(8,128)}), f32[768,768]{1,0:T(8,128)}) %all-gather.27.cloned.1.call-update) | async-done | bytes 2359312 | tf_op jit(solution)/shard_map/all_gather | solution.py:40
  706.7 0.0 all-gather.35.cloned.1.call-start
  706.7 37.3 %all-gather.33.cloned.1.call-done = f32[192,3072]{1,0:T(8,128)} async-done(((f32[96,3072]{1,0:T(8,128)}), f32[192,3072]{1,0:T(8,128)}) %all-gather.33.cloned.1.call-update) | async-done | bytes 2359312 | tf_op jit(solution)/shard_map/all_gather | solution.py:40
  744.0 15.5 %add_convert_fusion = bf16[2048,768]{1,0:T(8,128)(2,1)} fusion(bf16[2048,768]{1,0:T(8,128)(2,1)S(1)} %copy-done.6, bf16[2048,3072]{1,0:T(8,128)(2,1)} %fusion.17, bf16[768,3072]{1,0:T(8,128)(2,1)} %param.14), kind=kOutput, calls=%fused_computation.34 | convolution fusion | flops 9668395008 | bytes 23592960 | tf_op jit(solution)/shard_map/dot_general | solution.py:28
  759.5 50.5 %all-gather.17.cloned.1.call-done = f32[3072,768]{1,0:T(8,128)} async-done(((f32[768,768]{1,0:T(8,128)}), f32[3072,768]{1,0:T(8,128)}) %all-gather.17.cloned.1.call-update) | async-done | bytes 9437200 | tf_op jit(solution)/shard_map/all_gather | solution.py:41
  810.0 66.0 %all-gather.23.cloned.1.call-done = f32[768,3072]{1,0:T(8,128)} async-done(((f32[192,3072]{1,0:T(8,128)}), f32[768,3072]{1,0:T(8,128)}) %all-gather.23.cloned.1.call-update) | async-done | bytes 9437200 | tf_op jit(solution)/shard_map/all_gather | solution.py:41
  876.0 66.2 %all-gather.29.cloned.1.call-done = f32[3072,768]{1,0:T(8,128)} async-done(((f32[768,768]{1,0:T(8,128)}), f32[3072,768]{1,0:T(8,128)}) %all-gather.29.cloned.1.call-update) | async-done | bytes 9437200 | tf_op jit(solution)/shard_map/all_gather | solution.py:41
  942.1 66.0 %all-gather.35.cloned.1.call-done = f32[768,3072]{1,0:T(8,128)} async-done(((f32[192,3072]{1,0:T(8,128)}), f32[768,3072]{1,0:T(8,128)}) %all-gather.35.cloned.1.call-update) | async-done | bytes 9437200 | tf_op jit(solution)/shard_map/all_gather | solution.py:41
  1008.1 8.7 copy.18
  1016.8 4.8 copy.19
  1021.6 8.2 copy.20
  1029.9 3.7 copy.21
  (40 shorter events, 0.4 us)
Async XLA Ops:
  7.2 79.4 %copy-start = (bf16[2048,768]{1,0:T(8,128)(2,1)S(1)}, bf16[2048,768]{1,0:T(8,128)(2,1)}, u32[]{:S(2)}) copy-start(bf16[2048,768]{1,0:T(8,128)(2,1)} %param.11) | copy-start | bytes 9437188
  22.7 59.2 %all-to-all-start = ((bf16[4,768,768]{2,1,0:T(8,128)(2,1)}), bf16[4,768,768]{2,1,0:T(8,128)(2,1)}, u32[]{:S(2)}, u32[]{:S(2)}) async-start(bf16[4,768,768]{2,1,0:T(8,128)(2,1)} %bitcast.25), calls=%async_computation | async-start | bytes 9437184 | tf_op jit(solution)/shard_map/all_to_all | solution.py:35
  27.7 286.5 %reduce-scatter.9.cloned.1.call-start = ((), (), s32[]{:S(2)}) async-start(), calls=%async_computation.12 | async-start | bytes 3538944 | tf_op jit(solution)/shard_map/reduce_scatter | solution.py:37
  101.0 5.4 copy-start.3
  101.0 58.7 %all-to-all-start.1 = ((bf16[4,192,3072]{2,1,0:T(8,128)(2,1)}), bf16[4,192,3072]{2,1,0:T(8,128)(2,1)}, u32[]{:S(2)}, u32[]{:S(2)}) async-start(bf16[4,192,3072]{2,1,0:T(8,128)(2,1)} %bitcast.24), calls=%async_computation.3 | async-start | bytes 9437184 | tf_op jit(solution)/shard_map/all_to_all | solution.py:35
  106.2 208.6 %reduce-scatter.13.cloned.1.call-start = ((), (), s32[]{:S(2)}) async-start(), calls=%async_computation.17 | async-start | bytes 3538944 | tf_op jit(solution)/shard_map/reduce_scatter | solution.py:37
  121.9 42.7 %copy-start.5 = (bf16[2048,768]{1,0:T(8,128)(2,1)S(1)}, bf16[2048,768]{1,0:T(8,128)(2,1)}, u32[]{:S(2)}) copy-start(bf16[2048,768]{1,0:T(8,128)(2,1)} %add_convert_fusion.1) | copy-start | bytes 9437188
  179.1 58.5 %all-to-all-start.2 = ((bf16[4,768,768]{2,1,0:T(8,128)(2,1)}), bf16[4,768,768]{2,1,0:T(8,128)(2,1)}, u32[]{:S(2)}, u32[]{:S(2)}) async-start(bf16[4,768,768]{2,1,0:T(8,128)(2,1)} %bitcast.26), calls=%async_computation.6 | async-start | bytes 9437184 | tf_op jit(solution)/shard_map/all_to_all | solution.py:35
  184.0 131.4 %reduce-scatter.17.cloned.1.call-start = ((), (), s32[]{:S(2)}) async-start(), calls=%async_computation.22 | async-start | bytes 3538944 | tf_op jit(solution)/shard_map/reduce_scatter | solution.py:37
  206.6 35.8 %copy-start.4 = (bf16[2048,768]{1,0:T(8,128)(2,1)S(1)}, bf16[2048,768]{1,0:T(8,128)(2,1)}, u32[]{:S(2)}) copy-start(bf16[2048,768]{1,0:T(8,128)(2,1)} %param.9) | copy-start | bytes 9437188
  242.2 107.9 %reduce-scatter.21.cloned.1.call-start = ((), (), s32[]{:S(2)}) async-start(), calls=%async_computation.27 | async-start | bytes 3538944 | tf_op jit(solution)/shard_map/reduce_scatter | solution.py:37
  314.2 67.6 %reduce-scatter.11.cloned.1.call-start = ((), (), s32[]{:S(2)}) async-start(), calls=%async_computation.13 | async-start | bytes 1474560 | tf_op jit(solution)/shard_map/reduce_scatter | solution.py:38
  314.7 97.1 %reduce-scatter.15.cloned.1.call-start = ((), (), s32[]{:S(2)}) async-start(), calls=%async_computation.18 | async-start | bytes 1474560 | tf_op jit(solution)/shard_map/reduce_scatter | solution.py:38
  314.8 429.2 %copy-start.6 = (bf16[2048,768]{1,0:T(8,128)(2,1)S(1)}, bf16[2048,768]{1,0:T(8,128)(2,1)}, u32[]{:S(2)}) copy-start(bf16[2048,768]{1,0:T(8,128)(2,1)} %add_convert_fusion.1) | copy-start | bytes 9437188
  315.3 126.8 %reduce-scatter.19.cloned.1.call-start = ((), (), s32[]{:S(2)}) async-start(), calls=%async_computation.23 | async-start | bytes 1474560 | tf_op jit(solution)/shard_map/reduce_scatter | solution.py:38
  316.1 156.3 %reduce-scatter.23.cloned.1.call-start = ((), (), s32[]{:S(2)}) async-start(), calls=%async_computation.28 | async-start | bytes 1474560 | tf_op jit(solution)/shard_map/reduce_scatter | solution.py:38
  350.1 152.3 %all-gather.13.cloned.1.call-start = ((), (), s32[]{:S(2)}) async-start(), calls=%async_computation.14 | async-start | bytes 1474560 | tf_op jit(solution)/shard_map/all_gather | solution.py:39
  381.7 151.6 %all-gather.19.cloned.1.call-start = ((), (), s32[]{:S(2)}) async-start(), calls=%async_computation.19 | async-start | bytes 1474560 | tf_op jit(solution)/shard_map/all_gather | solution.py:39
  411.8 152.4 %all-gather.25.cloned.1.call-start = ((), (), s32[]{:S(2)}) async-start(), calls=%async_computation.24 | async-start | bytes 1474560 | tf_op jit(solution)/shard_map/all_gather | solution.py:39
  442.1 153.0 %all-gather.31.cloned.1.call-start = ((), (), s32[]{:S(2)}) async-start(), calls=%async_computation.29 | async-start | bytes 1474560 | tf_op jit(solution)/shard_map/all_gather | solution.py:39
  472.4 159.6 %all-gather.15.cloned.1.call-start = ((), (), s32[]{:S(2)}) async-start(), calls=%async_computation.15 | async-start | bytes 3538944 | tf_op jit(solution)/shard_map/all_gather | solution.py:40
  502.5 166.8 %all-gather.21.cloned.1.call-start = ((), (), s32[]{:S(2)}) async-start(), calls=%async_computation.20 | async-start | bytes 3538944 | tf_op jit(solution)/shard_map/all_gather | solution.py:40
  533.3 173.3 %all-gather.27.cloned.1.call-start = ((), (), s32[]{:S(2)}) async-start(), calls=%async_computation.25 | async-start | bytes 3538944 | tf_op jit(solution)/shard_map/all_gather | solution.py:40
  564.3 179.7 %all-gather.33.cloned.1.call-start = ((), (), s32[]{:S(2)}) async-start(), calls=%async_computation.30 | async-start | bytes 3538944 | tf_op jit(solution)/shard_map/all_gather | solution.py:40
  595.1 214.9 %all-gather.17.cloned.1.call-start = ((), (), s32[]{:S(2)}) async-start(), calls=%async_computation.16 | async-start | bytes 11796480 | tf_op jit(solution)/shard_map/all_gather | solution.py:41
  632.0 244.0 %all-gather.23.cloned.1.call-start = ((), (), s32[]{:S(2)}) async-start(), calls=%async_computation.21 | async-start | bytes 11796480 | tf_op jit(solution)/shard_map/all_gather | solution.py:41
  669.3 272.8 %all-gather.29.cloned.1.call-start = ((), (), s32[]{:S(2)}) async-start(), calls=%async_computation.26 | async-start | bytes 11796480 | tf_op jit(solution)/shard_map/all_gather | solution.py:41
  706.7 301.5 %all-gather.35.cloned.1.call-start = ((), (), s32[]{:S(2)}) async-start(), calls=%async_computation.31 | async-start | bytes 11796480 | tf_op jit(solution)/shard_map/all_gather | solution.py:41
  1008.1 8.7 copy-start.2
  1016.8 13.0 %slice-start = ((s8[9437184]{0:T(1024)(128)(4,1)}), s8[1048576]{0:T(1024)(128)(4,1)S(1)}, s32[]{:S(2)}) async-start(s8[9437184]{0:T(1024)(128)(4,1)} %bitcast.22), calls=%async_computation.32 | async-start | bytes 2097152
  1016.8 13.0 %slice-start.1 = ((s8[9437184]{0:T(1024)(128)(4,1)}), s8[4194304]{0:T(1024)(128)(4,1)S(1)}, s32[]{:S(2)}) async-start(s8[9437184]{0:T(1024)(128)(4,1)} %bitcast.22), calls=%async_computation.33 | async-start | bytes 8388608
  1021.6 8.3 slice-start.2
  1021.6 12.0 %copy-start.1 = (bf16[2048,768]{1,0:T(8,128)(2,1)S(1)}, bf16[2048,768]{1,0:T(8,128)(2,1)}, u32[]{:S(2)}) copy-start(bf16[2048,768]{1,0:T(8,128)(2,1)} %param.11) | copy-start | bytes 9437188
Sparse Core Ops, SparseCore 0:
  86.7 35.7 reduce-scatter.8
  164.7 35.7 reduce-scatter.12
  242.3 35.7 reduce-scatter.16
  314.3 35.7 reduce-scatter.20
  352.3 29.3 reduce-scatter.10
  383.9 27.8 reduce-scatter.14
  414.1 27.9 reduce-scatter.18
  444.4 27.9 reduce-scatter.22
  473.9 28.5 all-gather.12
  503.9 29.3 all-gather.18
  534.9 29.3 all-gather.24
  565.7 29.3 all-gather.30
  596.6 35.2 all-gather.14
  633.3 35.9 all-gather.20
  670.7 35.9 all-gather.26
  708.0 35.9 all-gather.32
  745.4 64.5 all-gather.16
  811.4 64.5 all-gather.22
  877.6 64.5 all-gather.28
  943.6 64.5 all-gather.34
where the time goes:
time: 1040 us
  waiting for transfers between devices  777 us (75%)
  matrix products  135 us (13%)
  blocking collectives  56.3 us (5%)
  local copies, waits for them, and re-layouts  25.5 us (2%)
  other arithmetic  16.4 us (2%)
  starting transfers between devices  16.3 us (2%)
  between operations  14.5 us (1%)
    all_gather x4, waiting for transfers between devices, reduce_grad(): return lax.all_gather(full_sum, 'group', axis=0, tiled=True)  249 us
    all_gather x4, waiting for transfers between devices, reduce_grad(): full_sum = lax.all_gather(full_sum, 'second', axis=0, tiled=True)  149 us
    all_gather x4, waiting for transfers between devices, reduce_grad(): full_sum = lax.all_gather(part_sum, 'third', axis=0, tiled=True)  122 us
    reduce_scatter x4, waiting for transfers between devices, reduce_grad(): lax.psum_scatter(part_sum, 'third', scatter_dimension=0, tiled=True)  122 us
    all_to_all x3, waiting for transfers between devices, reduce_grad(): received = lax.all_to_all(pieces, 'group', 0, 0)  99.3 us
    all_to_all x1, blocking collectives, reduce_grad(): received = lax.all_to_all(pieces, 'group', 0, 0)  56.3 us
    dot_general x2, matrix products, block_backward(): lax.dot_general(grad_y, w_out, CONTRACT_COLS, preferred_element_type=jnp....  46.1 us
    reduce_scatter x4, waiting for transfers between devices, reduce_grad(): lax.psum_scatter(part_sum, 'second', scatter_dimension=0, tiled=True)  34.1 us
  transfers between devices with their start and end apart: 23, of which 20 were waited for; matrix products, arithmetic and copies ran while one was open for 13% of the time, Pallas kernels for 0%

commit v1 on v0

--- a/solution.py
+++ b/solution.py
@@ -30,15 +30,8 @@
 
 
 def reduce_grad(grad, group_size):
-    row_count, col_count = grad.shape
-    pieces = grad.reshape(group_size, row_count // group_size, col_count)
-    received = lax.all_to_all(pieces, 'group', 0, 0)
-    part_sum = jnp.sum(received, axis=0, dtype=jnp.float32)
-    part_sum = lax.psum_scatter(part_sum, 'second', scatter_dimension=0, tiled=True)
-    part_sum = lax.psum_scatter(part_sum, 'third', scatter_dimension=0, tiled=True)
-    full_sum = lax.all_gather(part_sum, 'third', axis=0, tiled=True)
-    full_sum = lax.all_gather(full_sum, 'second', axis=0, tiled=True)
-    return lax.all_gather(full_sum, 'group', axis=0, tiled=True)
+    part_sum = lax.psum_scatter(grad.astype(jnp.float32), AXES, scatter_dimension=0, tiled=True)
+    return lax.all_gather(part_sum, AXES, axis=0, tiled=True)
 
 
 def solution(mesh):

time: 1040 us -> 1030 us (level)
  blocking collectives: 56.3 us -> 0 us
  waiting for transfers between devices: 777 us -> 825 us
  local copies, waits for them, and re-layouts: 25.5 us -> 48.1 us
  other arithmetic: 16.4 us -> 0.01 us
  starting transfers between devices: 16.3 us -> 0.32 us
    reduce_scatter x8 -> x4, waiting for transfers between devices: 156 us -> 508 us  [reduce_grad(): lax.psum_scatter(grad.astype(jnp.float32), AXES, scatter_dimension=0, til...]
    all_gather x12 -> x4, waiting for transfers between devices: 520 us -> 317 us  [reduce_grad(): return lax.all_gather(part_sum, AXES, axis=0, tiled=True)]
    all_to_all x3 -> x0, waiting for transfers between devices: 99.3 us -> none  [reduce_grad(): received = lax.all_to_all(pieces, 'group', 0, 0)]
    all_to_all x1 -> x0, blocking collectives: 56.3 us -> none  [reduce_grad(): received = lax.all_to_all(pieces, 'group', 0, 0)]
    unnamed x24 -> x28, local copies, waits for them, and re-layouts: 25.5 us -> 48.1 us
    reduce_sum x4 -> x0, other arithmetic: 16.4 us -> none  [reduce_grad(): part_sum = jnp.sum(received, axis=0, dtype=jnp.float32)]
    all_to_all x3 -> x0, starting transfers between devices: 15.1 us -> none  [reduce_grad(): received = lax.all_to_all(pieces, 'group', 0, 0)]
  transfers between devices with their start and end apart: 23 -> 8, of which waited for: 20 -> 8; matrix products, arithmetic and copies ran while one was open for 13% -> 7% of each run, Pallas kernels for 0% -> 0%
where the time goes in v1:
time: 1030 us
  waiting for transfers between devices  825 us (80%)
  matrix products  141 us (14%)
  local copies, waits for them, and re-layouts  48.1 us (5%)
  between operations  14.2 us (1%)
    reduce_scatter x4, waiting for transfers between devices, reduce_grad(): lax.psum_scatter(grad.astype(jnp.float32), AXES, scatter_dimension=0, til...  508 us
    all_gather x4, waiting for transfers between devices, reduce_grad(): return lax.all_gather(part_sum, AXES, axis=0, tiled=True)  317 us
    unnamed x28, local copies, waits for them, and re-layouts  48.1 us
    dot_general x2, matrix products, block_backward(): lax.dot_general(grad_y, w_out, CONTRACT_COLS, preferred_element_type=jnp....  47 us
    dot_general x2, matrix products, block_backward(): lax.dot_general(grad_pre, w_in, CONTRACT_COLS, preferred_element_type=jnp...  31.8 us
    dot_general x2, matrix products, block_backward(): lax.dot_general(hidden, grad_y, CONTRACT_ROWS, preferred_element_type=jnp...  31.3 us
    dot_general x2, matrix products, block_backward(): lax.dot_general(x_in, grad_pre, CONTRACT_ROWS, preferred_element_type=jnp...  30.7 us
  transfers between devices with their start and end apart: 8, of which 8 were waited for; matrix products, arithmetic and copies ran while one was open for 7% of the time, Pallas kernels for 0%

profile of v1, /device:TPU:0, one launch (start us, length us, event | category | flops | bytes accessed | tf_op | source)
XLA Modules:
  0.0 1028.5 jit_solution(6345029198704749084)
XLA Ops:
  7.2 0.0 copy-start
  7.2 0.0 reduce-scatter.15.cloned.1.call-start
  7.2 0.0 copy-start.3
  7.2 0.0 slice-start.3
  7.3 0.0 slice-start.4
  7.3 24.1 %fusion.8 = bf16[2048,3072]{1,0:T(8,128)(2,1)} fusion(bf16[2048,3072]{1,0:T(8,128)(2,1)} %param.12, bf16[2048,768]{1,0:T(8,128)(2,1)} %param.13, bf16[3072,768]{1,0:T(8,128)(2,1)} %param.17), kind=kOutput, calls=%fused_computation.18 | convolution fusion | flops 9732882432 | bytes 33030144 | tf_op jit(solution)/shard_map/dot_general | solution.py:25
  31.4 0.0 copy-done.3
  31.4 0.0 slice-start.5
  31.4 15.6 %add_convert_fusion.1 = bf16[2048,768]{1,0:T(8,128)(2,1)} fusion(bf16[2048,768]{1,0:T(8,128)(2,1)S(1)} %copy-done.3, bf16[2048,3072]{1,0:T(8,128)(2,1)} %fusion.8, bf16[768,3072]{1,0:T(8,128)(2,1)} %param.16), kind=kOutput, calls=%fused_computation.33 | convolution fusion | flops 9668395008 | bytes 23592960 | tf_op jit(solution)/shard_map/dot_general | solution.py:28
  47.0 0.0 slice-done.3
  47.0 0.0 slice-done.4
  47.0 0.0 slice-done.5
  47.0 22.9 %fusion.17 = bf16[2048,3072]{1,0:T(8,128)(2,1)} fusion(bf16[2048,3072]{1,0:T(8,128)(2,1)S(1)} %bitcast.23, bf16[2048,768]{1,0:T(8,128)(2,1)} %add_convert_fusion.1, bf16[3072,768]{1,0:T(8,128)(2,1)} %param.15), kind=kOutput, calls=%fused_computation.27 | convolution fusion | flops 9732882432 | bytes 33030144 | tf_op jit(solution)/shard_map/dot_general | solution.py:25
  69.9 0.0 copy-done
  69.9 15.2 %convert_bitcast_fusion = f32[768,3072]{0,1:T(8,128)} fusion(bf16[2048,3072]{1,0:T(8,128)(2,1)} %fusion.17, bf16[2048,768]{1,0:T(8,128)(2,1)S(1)} %copy-done), kind=kOutput, calls=%fused_computation.30 | convolution fusion | flops 9668395008 | bytes 25165824 | tf_op jit(solution)/shard_map/dot_general | solution.py:27
  85.1 9.6 copy.20
  94.7 0.0 reduce-scatter.15.cloned.1.call-update
  94.7 0.0 copy-start.2
  94.7 0.0 reduce-scatter.11.cloned.1.call-start
  94.8 16.2 %fusion.28 = f32[3072,768]{1,0:T(8,128)} fusion(bf16[2048,768]{1,0:T(8,128)(2,1)} %add_convert_fusion.1, bf16[2048,3072]{1,0:T(8,128)(2,1)} %param.10), kind=kOutput, calls=%fused_computation.38 | convolution fusion | flops 9706143744 | bytes 25165824 | tf_op jit(solution)/shard_map/dot_general | solution.py:24
  111.0 0.0 reduce-scatter.11.cloned.1.call-update
  111.0 0.0 reduce-scatter.13.cloned.1.call-start
  111.0 0.0 copy-done.2
  111.1 15.5 %convert_bitcast_fusion.1 = f32[768,3072]{0,1:T(8,128)} fusion(bf16[2048,3072]{1,0:T(8,128)(2,1)} %fusion.8, bf16[2048,768]{1,0:T(8,128)(2,1)S(1)} %copy-done.2), kind=kOutput, calls=%fused_computation.31 | convolution fusion | flops 9668395008 | bytes 25165824 | tf_op jit(solution)/shard_map/dot_general | solution.py:27
  126.5 0.0 copy-start.4
  126.5 9.7 copy.18
  136.3 0.0 reduce-scatter.13.cloned.1.call-update
  136.3 0.0 reduce-scatter.9.cloned.1.call-start
  136.3 0.0 copy-done.4
  136.3 15.1 %fusion.31 = f32[3072,768]{1,0:T(8,128)} fusion(bf16[2048,768]{1,0:T(8,128)(2,1)S(1)} %copy-done.4, bf16[2048,3072]{1,0:T(8,128)(2,1)} %param.12), kind=kOutput, calls=%fused_computation.39 | convolution fusion | flops 9706143744 | bytes 25165824 | tf_op jit(solution)/shard_map/dot_general | solution.py:24
  151.5 0.0 reduce-scatter.9.cloned.1.call-update
  151.5 0.0 all-gather.11.cloned.1.call-start
  151.5 82.4 %reduce-scatter.15.cloned.1.call-done = f32[24,3072]{1,0:T(8,128)} async-done(((f32[768,3072]{1,0:T(8,128)}), f32[24,3072]{1,0:T(8,128)}) %reduce-scatter.15.cloned.1.call-update) | async-done | bytes 294928 | tf_op jit(solution)/shard_map/reduce_scatter | solution.py:33
  233.9 0.0 all-gather.11.cloned.1.call-update
  233.9 0.0 all-gather.9.cloned.1.call-start
  234.0 141.9 %reduce-scatter.11.cloned.1.call-done = f32[96,768]{1,0:T(8,128)} async-done(((f32[3072,768]{1,0:T(8,128)}), f32[96,768]{1,0:T(8,128)}) %reduce-scatter.11.cloned.1.call-update) | async-done | bytes 294928 | tf_op jit(solution)/shard_map/reduce_scatter | solution.py:33
  375.9 0.0 all-gather.9.cloned.1.call-update
  375.9 0.0 all-gather.7.cloned.1.call-start
  375.9 141.9 %reduce-scatter.13.cloned.1.call-done = f32[24,3072]{1,0:T(8,128)} async-done(((f32[768,3072]{1,0:T(8,128)}), f32[24,3072]{1,0:T(8,128)}) %reduce-scatter.13.cloned.1.call-update) | async-done | bytes 294928 | tf_op jit(solution)/shard_map/reduce_scatter | solution.py:33
  517.8 0.0 all-gather.7.cloned.1.call-update
  517.8 0.0 all-gather.5.cloned.1.call-start
  517.9 141.6 %reduce-scatter.9.cloned.1.call-done = f32[96,768]{1,0:T(8,128)} async-done(((f32[3072,768]{1,0:T(8,128)}), f32[96,768]{1,0:T(8,128)}) %reduce-scatter.9.cloned.1.call-update) | async-done | bytes 294928 | tf_op jit(solution)/shard_map/reduce_scatter | solution.py:33
  659.5 0.0 all-gather.5.cloned.1.call-update
  659.5 16.2 %add_convert_fusion = bf16[2048,768]{1,0:T(8,128)(2,1)} fusion(bf16[2048,768]{1,0:T(8,128)(2,1)} %add_convert_fusion.1, bf16[2048,3072]{1,0:T(8,128)(2,1)} %fusion.17, bf16[768,3072]{1,0:T(8,128)(2,1)} %param.14), kind=kOutput, calls=%fused_computation.32 | convolution fusion | flops 9668395008 | bytes 23592960 | tf_op jit(solution)/shard_map/dot_general | solution.py:28
  675.7 67.2 %all-gather.11.cloned.1.call-done = f32[768,3072]{1,0:T(8,128)} async-done(((f32[24,3072]{1,0:T(8,128)}), f32[768,3072]{1,0:T(8,128)}) %all-gather.11.cloned.1.call-update) | async-done | bytes 9437200 | tf_op jit(solution)/shard_map/all_gather | solution.py:34
  742.9 83.2 %all-gather.9.cloned.1.call-done = f32[3072,768]{1,0:T(8,128)} async-done(((f32[96,768]{1,0:T(8,128)}), f32[3072,768]{1,0:T(8,128)}) %all-gather.9.cloned.1.call-update) | async-done | bytes 9437200 | tf_op jit(solution)/shard_map/all_gather | solution.py:34
  826.2 83.4 %all-gather.7.cloned.1.call-done = f32[768,3072]{1,0:T(8,128)} async-done(((f32[24,3072]{1,0:T(8,128)}), f32[768,3072]{1,0:T(8,128)}) %all-gather.7.cloned.1.call-update) | async-done | bytes 9437200 | tf_op jit(solution)/shard_map/all_gather | solution.py:34
  909.5 83.4 %all-gather.5.cloned.1.call-done = f32[3072,768]{1,0:T(8,128)} async-done(((f32[96,768]{1,0:T(8,128)}), f32[3072,768]{1,0:T(8,128)}) %all-gather.5.cloned.1.call-update) | async-done | bytes 9437200 | tf_op jit(solution)/shard_map/all_gather | solution.py:34
  992.9 8.0 copy.26
  1000.9 0.0 slice-start
  1000.9 0.0 slice-start.1
  1000.9 8.8 copy.27
  1009.7 0.0 slice-start.2
  1009.7 0.0 copy-start.1
  1009.7 8.2 copy.28
  1017.9 0.0 slice-done
  1017.9 0.0 slice-done.1
  1017.9 0.0 slice-done.2
  1017.9 3.7 copy.29
  1021.6 0.0 copy-done.1
  (2 shorter events, 0.0 us)
Async XLA Ops:
  7.2 62.7 %copy-start = (bf16[2048,768]{1,0:T(8,128)(2,1)S(1)}, bf16[2048,768]{1,0:T(8,128)(2,1)}, u32[]{:S(2)}) copy-start(bf16[2048,768]{1,0:T(8,128)(2,1)} %param.9) | copy-start | bytes 9437188
  7.2 226.7 %reduce-scatter.15.cloned.1.call-start = ((), (), s32[]{:S(2)}) async-start(), calls=%async_computation.11 | async-start | bytes 9732096 | tf_op jit(solution)/shard_map/reduce_scatter | solution.py:33
  7.2 24.1 %copy-start.3 = (bf16[2048,768]{1,0:T(8,128)(2,1)S(1)}, bf16[2048,768]{1,0:T(8,128)(2,1)}, u32[]{:S(2)}) copy-start(bf16[2048,768]{1,0:T(8,128)(2,1)} %param.13) | copy-start | bytes 9437188
  7.2 39.7 %slice-start.3 = ((s8[12582912]{0:T(1024)(128)(4,1)}), s8[4194304]{0:T(1024)(128)(4,1)S(1)}, s32[]{:S(2)}) async-start(s8[12582912]{0:T(1024)(128)(4,1)} %bitcast.22), calls=%async_computation.15 | async-start | bytes 8388608
  7.3 39.7 %slice-start.4 = ((s8[12582912]{0:T(1024)(128)(4,1)}), s8[4194304]{0:T(1024)(128)(4,1)S(1)}, s32[]{:S(2)}) async-start(s8[12582912]{0:T(1024)(128)(4,1)} %bitcast.22), calls=%async_computation.16 | async-start | bytes 8388608
  31.4 15.6 %slice-start.5 = ((s8[12582912]{0:T(1024)(128)(4,1)}), s8[4194304]{0:T(1024)(128)(4,1)S(1)}, s32[]{:S(2)}) async-start(s8[12582912]{0:T(1024)(128)(4,1)} %bitcast.22), calls=%async_computation.17 | async-start | bytes 8388608
  94.7 16.3 %copy-start.2 = (bf16[2048,768]{1,0:T(8,128)(2,1)S(1)}, bf16[2048,768]{1,0:T(8,128)(2,1)}, u32[]{:S(2)}) copy-start(bf16[2048,768]{1,0:T(8,128)(2,1)} %param.11) | copy-start | bytes 9437188
  94.7 281.1 %reduce-scatter.11.cloned.1.call-start = ((), (), s32[]{:S(2)}) async-start(), calls=%async_computation.7 | async-start | bytes 9732096 | tf_op jit(solution)/shard_map/reduce_scatter | solution.py:33
  111.0 406.8 %reduce-scatter.13.cloned.1.call-start = ((), (), s32[]{:S(2)}) async-start(), calls=%async_computation.10 | async-start | bytes 9732096 | tf_op jit(solution)/shard_map/reduce_scatter | solution.py:33
  126.5 9.8 copy-start.4
  136.3 523.2 %reduce-scatter.9.cloned.1.call-start = ((), (), s32[]{:S(2)}) async-start(), calls=%async_computation.4 | async-start | bytes 9732096 | tf_op jit(solution)/shard_map/reduce_scatter | solution.py:33
  151.5 591.4 %all-gather.11.cloned.1.call-start = ((), (), s32[]{:S(2)}) async-start(), calls=%async_computation.9 | async-start | bytes 9732096 | tf_op jit(solution)/shard_map/all_gather | solution.py:34
  233.9 592.2 %all-gather.9.cloned.1.call-start = ((), (), s32[]{:S(2)}) async-start(), calls=%async_computation.8 | async-start | bytes 9732096 | tf_op jit(solution)/shard_map/all_gather | solution.py:34
  375.9 533.6 %all-gather.7.cloned.1.call-start = ((), (), s32[]{:S(2)}) async-start(), calls=%async_computation.6 | async-start | bytes 9732096 | tf_op jit(solution)/shard_map/all_gather | solution.py:34
  517.8 475.0 %all-gather.5.cloned.1.call-start = ((), (), s32[]{:S(2)}) async-start(), calls=%async_computation.5 | async-start | bytes 9732096 | tf_op jit(solution)/shard_map/all_gather | solution.py:34
  1000.9 17.0 %slice-start = ((s8[9437184]{0:T(1024)(128)(4,1)}), s8[4194304]{0:T(1024)(128)(4,1)S(1)}, s32[]{:S(2)}) async-start(s8[9437184]{0:T(1024)(128)(4,1)} %bitcast.20), calls=%async_computation.12 | async-start | bytes 8388608
  1000.9 17.0 %slice-start.1 = ((s8[9437184]{0:T(1024)(128)(4,1)}), s8[4194304]{0:T(1024)(128)(4,1)S(1)}, s32[]{:S(2)}) async-start(s8[9437184]{0:T(1024)(128)(4,1)} %bitcast.20), calls=%async_computation.13 | async-start | bytes 8388608
  1009.7 8.2 slice-start.2
  1009.7 12.0 %copy-start.1 = (bf16[2048,768]{1,0:T(8,128)(2,1)S(1)}, bf16[2048,768]{1,0:T(8,128)(2,1)}, u32[]{:S(2)}) copy-start(bf16[2048,768]{1,0:T(8,128)(2,1)} %param.9) | copy-start | bytes 9437188
Sparse Core Ops, SparseCore 0:
  94.8 138.9 reduce-scatter.14
  240.4 135.4 reduce-scatter.10
  382.4 135.4 reduce-scatter.12
  524.2 135.3 reduce-scatter.8
  662.2 80.6 all-gather.10
  745.7 80.4 all-gather.8
  829.0 80.4 all-gather.6
  912.4 80.4 all-gather.4

commit v2 on v1

--- a/solution.py
+++ b/solution.py
@@ -1,7 +1,11 @@
+import functools
+import heapq
 import math
 import jax
 import jax.numpy as jnp
 from jax import lax
+from jax.experimental import pallas as pl
+from jax.experimental.pallas import tpu as pltpu
 from jax.sharding import PartitionSpec as P
 
 AXES = ('third', 'second', 'group')
@@ -29,22 +33,176 @@
     return w_out_grad, w_in_grad, grad_x
 
 
-def reduce_grad(grad, group_size):
-    part_sum = lax.psum_scatter(grad.astype(jnp.float32), AXES, scatter_dimension=0, tiled=True)
-    return lax.all_gather(part_sum, AXES, axis=0, tiled=True)
+MESH = pl.DeviceIdType.MESH
+CHUNKS = 2
+STAGES = (('x', 'a', 'y', 'b'), ('y', 'a', 'x', 'b'))
+LINK_NS_PER_BYTE = 1.0 / 46.6
+
+
+def event_order(unit, width):
+    chunks = [(g, j, c) for g in range(4) for j in range(CHUNKS) for c in range(2)]
+    free = {'x': 0.0, 'y': 0.0, 'z': 0.0}
+    heap = [(800.0 * (i + 1), i, 0) for i in range(len(chunks))]
+    heapq.heapify(heap)
+    order, now = [], 0.0
+    while heap:
+        when, i, stage = heapq.heappop(heap)
+        now = max(now, when) + 300.0
+        order.append((i, chunks[i], stage))
+        if stage == 8:
+            continue
+        level = stage if stage < 4 else 7 - stage
+        axis = STAGES[chunks[i][2]][level]
+        link = 'z' if axis in 'ab' else axis
+        size = (unit >> (level + 1)) * width * 4
+        start = max(free[link], now)
+        free[link] = start + size * LINK_NS_PER_BYTE
+        heapq.heappush(heap, (free[link] + 2000.0, i, stage + 1))
+    return chunks, order
+
+
+def reduce_kernel(unit, width, *refs):
+    grads, outs = refs[:4], refs[4:8]
+    acc, own, rec_d, rec0, rec1, rec2, rec3, own_sem, send_sem, recv_sem, out_sem, free_sem = refs[8:]
+    recs = (rec0, rec1, rec2, rec3)
+    chunks, order = event_order(unit, width)
+    group, second, third = lax.axis_index('group'), lax.axis_index('second'), lax.axis_index('third')
+    core = group % 2
+    peers = {
+        'd': {'group': group + 1 - 2 * core},
+        'x': {'group': (group + 2) % 4},
+        'y': {'second': 1 - second},
+        'a': {'third': third + 1 - 2 * (third % 2)},
+        'b': {'third': (third + 2) % 4},
+    }
+    bits = {'x': group // 2, 'y': second, 'a': third % 2, 'b': third // 2}
+
+    barrier = pltpu.get_barrier_semaphore()
+    for peer in peers.values():
+        pl.semaphore_signal(barrier, inc=1, device_id=peer, device_id_type=MESH)
+    pl.semaphore_wait(barrier, len(peers))
+
+    def window(ref, chunk, half):
+        g, j, c = chunk
+        if g % 2 == 0:
+            return ref.at[pl.ds(half * 2 * unit + c * unit, unit), pl.ds(j * width, width)]
+        return ref.at[pl.ds(0, unit), pl.ds(pl.multiple_of(half * 2 * unit + c * unit + j * width, 128), width)]
+
+    def remote(src, dst, i, k, axis):
+        return pltpu.make_async_remote_copy(
+            src_ref=src, dst_ref=dst, send_sem=send_sem.at[i, k], recv_sem=recv_sem.at[i, k],
+            device_id=peers[axis], device_id_type=MESH)
+
+    own_copy, copies = {}, {}
+    for i, chunk in enumerate(chunks):
+        grad = grads[chunk[0]]
+        own_copy[i] = pltpu.make_async_copy(window(grad, chunk, core), own.at[i], own_sem.at[i])
+        own_copy[i].start()
+        copies[i, 0] = remote(window(grad, chunk, 1 - core), rec_d.at[i], i, 0, 'd')
+        copies[i, 0].start()
+
+    def offsets(c):
+        offs = [0]
+        for k in range(4):
+            offs.append(offs[-1] + bits[STAGES[c][k]] * (unit >> (k + 1)))
+        return offs
+
+    offs_of = (offsets(0), offsets(1))
+
+    def rows_loop(count, fn):
+        block = math.gcd(count, 32)
+
+        @pl.loop(0, count // block)
+        def _(t):
+            fn(pl.multiple_of(t * block, 16), block)
+
+    for i, chunk, stage in order:
+        c = chunk[2]
+        offs = offs_of[c]
+        copies[i, stage].wait_recv()
+        if stage == 0:
+            own_copy[i].wait()
+
+            def first(base, i=i):
+                def fn(r, block):
+                    rows = pl.ds(pl.multiple_of(base + r, 16), block)
+                    acc[i, rows, :] = own[i, rows, :].astype(jnp.float32) + rec_d[i, rows, :].astype(jnp.float32)
+                return fn
+
+            bit = bits[STAGES[c][0]]
+            rows_loop(unit // 2, first((1 - bit) * (unit // 2)))
+        elif stage <= 4:
+            keep = offs[stage]
+
+            def add(r, block, i=i, keep=keep, rec=recs[stage - 1]):
+                rows = pl.ds(pl.multiple_of(keep + r, 16), block)
+                acc[i, rows, :] += rec[i, pl.ds(r, block), :]
+
+            rows_loop(unit >> stage, add)
+            copies[i, stage].wait_send()
+            pl.semaphore_signal(free_sem.at[i, stage - 1], inc=1, device_id=peers[STAGES[c][stage - 1]], device_id_type=MESH)
+        if stage < 4:
+            half = unit >> (stage + 1)
+            other = pl.multiple_of(offs[stage] + (1 - bits[STAGES[c][stage]]) * half, 16)
+            copies[i, stage + 1] = remote(acc.at[i, pl.ds(other, half), :], recs[stage].at[i], i, stage + 1, STAGES[c][stage])
+            copies[i, stage + 1].start()
+            if stage == 0:
+                rows_loop(unit // 2, first(bit * (unit // 2)))
+        elif stage < 8:
+            level = 7 - stage
+            pl.semaphore_wait(free_sem.at[i, level], 1)
+            rows = pl.ds(pl.multiple_of(offs[level + 1], 16), unit >> (level + 1))
+            copies[i, stage + 1] = remote(acc.at[i, rows, :], acc.at[i, rows, :], i, stage + 1, STAGES[c][level])
+            copies[i, stage + 1].start()
+        else:
+            dst = window(outs[chunk[0]], chunk, core)
+            copies[i, 9] = remote(acc.at[i], dst, i, 9, 'd')
+            copies[i, 9].start()
+            pltpu.make_async_copy(acc.at[i], dst, out_sem.at[i]).start()
+
+    for i, chunk in enumerate(chunks):
+        for k in (0, 5, 6, 7, 8):
+            copies[i, k].wait_send()
+        copies[i, 9].wait()
+        pltpu.make_async_copy(acc.at[i], window(outs[chunk[0]], chunk, core), out_sem.at[i]).wait()
+
+
+def reduce_grads(grads):
+    unit = grads[0].shape[1]
+    width = unit // CHUNKS
+    count = 4 * CHUNKS * 2
+    any_spec = pl.BlockSpec(memory_space=pl.ANY)
+    return pl.pallas_call(
+        functools.partial(reduce_kernel, unit, width),
+        name='reduce_grads',
+        out_shape=[jax.ShapeDtypeStruct(grad.shape, jnp.float32) for grad in grads],
+        in_specs=[any_spec] * 4,
+        out_specs=[any_spec] * 4,
+        scratch_shapes=[
+            pltpu.VMEM((count, unit, width), jnp.float32),
+            pltpu.VMEM((count, unit, width), jnp.bfloat16),
+            pltpu.VMEM((count, unit, width), jnp.bfloat16),
+            pltpu.VMEM((count, unit // 2, width), jnp.float32),
+            pltpu.VMEM((count, unit // 4, width), jnp.float32),
+            pltpu.VMEM((count, unit // 8, width), jnp.float32),
+            pltpu.VMEM((count, unit // 16, width), jnp.float32),
+            pltpu.SemaphoreType.DMA((count,)),
+            pltpu.SemaphoreType.DMA((count, 10)),
+            pltpu.SemaphoreType.DMA((count, 10)),
+            pltpu.SemaphoreType.DMA((count,)),
+            pltpu.SemaphoreType.REGULAR((count, 4)),
+        ],
+        compiler_params=pltpu.CompilerParams(
+            collective_id=0, has_side_effects=True, vmem_limit_bytes=62 * 1024 * 1024),
+    )(*grads)
 
 
 def solution(mesh):
-    group_size = mesh.shape['group']
-
     def device_step(x_one, z_one, x_two, z_two, grad_out, w1_in, w1_out, w2_in, w2_out):
         w2o_grad, w2i_grad, dx_two = block_backward(x_two, z_two, grad_out, w2_in, w2_out)
-        sum_w2o = reduce_grad(w2o_grad, group_size)
-        sum_w2i = reduce_grad(w2i_grad, group_size)
         w1o_grad, w1i_grad, dx_one = block_backward(x_one, z_one, dx_two, w1_in, w1_out)
-        sum_w1o = reduce_grad(w1o_grad, group_size)
-        sum_w1i = reduce_grad(w1i_grad, group_size)
-        return sum_w2o, sum_w2i, sum_w1o, sum_w1i, dx_one
+        sums = reduce_grads([w2o_grad, w2i_grad, w1o_grad, w1i_grad])
+        return sums[0], sums[1], sums[2], sums[3], dx_one
 
     row_spec = P(AXES, None)
     repl_spec = P()

time: 1030 us -> 493 us (0.48)
  waiting for transfers between devices: 825 us -> 0 us
  Pallas kernels: 0 us -> 338 us
  local copies, waits for them, and re-layouts: 48.1 us -> 24.7 us
  between operations: 14.2 us -> 0.81 us
  matrix products: 141 us -> 129 us
    reduce_scatter x4 -> x0, waiting for transfers between devices: 508 us -> none  [reduce_grad(): lax.psum_scatter(grad.astype(jnp.float32), AXES, scatter_dimension=0, til...]
    pallas_call x0 -> x1, Pallas kernels: none -> 338 us  [reduce_grads(): pl.pallas_call(functools.partial(reduce_kernel, unit, width), name='reduc...]
    all_gather x4 -> x0, waiting for transfers between devices: 317 us -> none  [reduce_grad(): return lax.all_gather(part_sum, AXES, axis=0, tiled=True)]
    unnamed x28 -> x44, local copies, waits for them, and re-layouts: 48.1 us -> 24.7 us
  transfers between devices with their start and end apart: 8 -> 0, of which waited for: 8 -> 0; matrix products, arithmetic and copies ran while one was open for 7% -> 0% of each run, Pallas kernels for 0% -> 0%
where the time goes in v2:
time: 493 us
  Pallas kernels  338 us (69%)
  matrix products  129 us (26%)
  local copies, waits for them, and re-layouts  24.7 us (5%)
    pallas_call x1, Pallas kernels, reduce_grads(): pl.pallas_call(functools.partial(reduce_kernel, unit, width), name='reduc...  338 us
    dot_general x2, matrix products, block_backward(): lax.dot_general(grad_y, w_out, CONTRACT_COLS, preferred_element_type=jnp....  37.3 us
    dot_general x2, matrix products, block_backward(): lax.dot_general(hidden, grad_y, CONTRACT_ROWS, preferred_element_type=jnp...  32.8 us
    dot_general x2, matrix products, block_backward(): lax.dot_general(x_in, grad_pre, CONTRACT_ROWS, preferred_element_type=jnp...  30.1 us
    dot_general x2, matrix products, block_backward(): lax.dot_general(grad_pre, w_in, CONTRACT_COLS, preferred_element_type=jnp...  29 us
    unnamed x44, local copies, waits for them, and re-layouts  24.7 us

profile of v2, /device:TPU:0, one launch (start us, length us, event | category | flops | bytes accessed | tf_op | source)
XLA Modules:
  0.0 492.7 jit_solution(8131371154240363378)
XLA Ops:
  0.6 0.0 copy-start.2
  0.6 0.0 copy-start
  0.7 0.0 copy-start.1
  0.7 0.0 slice-start.9
  0.7 17.3 %fusion.22.refs_0_ = bf16[3072,768]{1,0:T(8,128)(2,1)} fusion(bf16[2048,768]{1,0:T(8,128)(2,1)} %param.13, bf16[2048,3072]{1,0:T(8,128)(2,1)} %param.12), kind=kOutput, calls=%fused_computation.32 | convolution fusion | flops 9703784448 | bytes 20447232 | tf_op jit(solution)/shard_map/dot_general | solution.py:28
  18.0 0.0 copy-done.2
  18.0 0.0 copy-done
  18.0 0.0 copy-done.1
  18.0 0.0 slice-start.10
  18.0 18.8 %fusion.8 = bf16[2048,3072]{1,0:T(8,128)(2,1)} fusion(bf16[2048,3072]{1,0:T(8,128)(2,1)S(1)} %copy-done, bf16[2048,768]{1,0:T(8,128)(2,1)S(1)} %copy-done.2, bf16[3072,768]{1,0:T(8,128)(2,1)S(1)} %copy-done.1), kind=kOutput, calls=%fused_computation.18 | convolution fusion | flops 9732882432 | bytes 33030144 | tf_op jit(solution)/shard_map/dot_general | solution.py:29
  36.8 0.0 slice-done.9
  36.8 0.0 slice-done.10
  36.8 0.0 slice-start.6
  36.8 0.0 slice-start.7
  36.8 0.0 slice-start.11
  36.8 14.3 %add_convert_fusion.1 = bf16[2048,768]{1,0:T(8,128)(2,1)} fusion(bf16[2048,768]{1,0:T(8,128)(2,1)S(1)} %copy-done.2, bf16[2048,3072]{1,0:T(8,128)(2,1)} %fusion.8, bf16[768,3072]{1,0:T(8,128)(2,1)S(1)} %bitcast.25), kind=kOutput, calls=%fused_computation.31 | convolution fusion | flops 9668395008 | bytes 23592960 | tf_op jit(solution)/shard_map/dot_general | solution.py:32
  51.1 0.0 slice-start.8
  51.1 0.0 slice-start.12
  51.1 15.5 %fusion.28.refs_1_ = bf16[768,3072]{1,0:T(8,128)(2,1)} fusion(bf16[2048,3072]{1,0:T(8,128)(2,1)} %fusion.8, bf16[2048,768]{1,0:T(8,128)(2,1)} %param.11), kind=kOutput, calls=%fused_computation.36 | convolution fusion | flops 9666035712 | bytes 20447232 | tf_op jit(solution)/shard_map/dot_general | solution.py:31
  66.6 0.0 slice-done.6
  66.6 0.0 slice-done.7
  66.6 0.0 slice-done.8
  66.6 0.0 copy-start.4
  66.6 0.0 slice-start.13
  66.6 15.5 %fusion.25.refs_2_ = bf16[3072,768]{1,0:T(8,128)(2,1)} fusion(bf16[2048,768]{1,0:T(8,128)(2,1)} %add_convert_fusion.1, bf16[2048,3072]{1,0:T(8,128)(2,1)S(1)} %bitcast.23), kind=kOutput, calls=%fused_computation.33 | convolution fusion | flops 9703784448 | bytes 20447232 | tf_op jit(solution)/shard_map/dot_general | solution.py:28
  82.1 0.0 slice-done.11
  82.1 0.0 slice-done.12
  82.1 0.0 copy-done.4
  82.2 0.0 slice-start.14
  82.2 18.5 %fusion.17 = bf16[2048,3072]{1,0:T(8,128)(2,1)} fusion(bf16[2048,3072]{1,0:T(8,128)(2,1)S(1)} %bitcast.23, bf16[2048,768]{1,0:T(8,128)(2,1)S(1)} %copy-done.4, bf16[3072,768]{1,0:T(8,128)(2,1)S(1)} %bitcast.27), kind=kOutput, calls=%fused_computation.27 | convolution fusion | flops 9732882432 | bytes 33030144 | tf_op jit(solution)/shard_map/dot_general | solution.py:29
  100.7 0.0 slice-done.13
  100.7 0.0 slice-done.14
  100.7 0.0 copy-start.3
  100.7 14.7 %add_convert_fusion = bf16[2048,768]{1,0:T(8,128)(2,1)} fusion(bf16[2048,768]{1,0:T(8,128)(2,1)} %add_convert_fusion.1, bf16[2048,3072]{1,0:T(8,128)(2,1)} %fusion.17, bf16[768,3072]{1,0:T(8,128)(2,1)S(1)} %bitcast.29), kind=kOutput, calls=%fused_computation.30 | convolution fusion | flops 9668395008 | bytes 23592960 | tf_op jit(solution)/shard_map/dot_general | solution.py:32
  115.4 0.0 copy-done.3
  115.4 14.6 %fusion.29.refs_3_ = bf16[768,3072]{1,0:T(8,128)(2,1)} fusion(bf16[2048,3072]{1,0:T(8,128)(2,1)} %fusion.17, bf16[2048,768]{1,0:T(8,128)(2,1)S(1)} %copy-done.3), kind=kOutput, calls=%fused_computation.37 | convolution fusion | flops 9666035712 | bytes 20447232 | tf_op jit(solution)/shard_map/dot_general | solution.py:31
  130.1 337.9 %reduce_grads.1 = (f32[3072,768]{1,0:T(8,128)}, f32[768,3072]{1,0:T(8,128)}, f32[3072,768]{1,0:T(8,128)}, f32[768,3072]{1,0:T(8,128)}) custom-call(bf16[3072,768]{1,0:T(8,128)(2,1)} %fusion.22.refs_0_, bf16[768,3072]{1,0:T(8,128)(2,1)} %fusion.28.refs_1_, bf16[3072,768]{1,0:T(8,128)(2,1)} %fusion.25.refs_2_, bf16[768,3072]{1,0:T(8,128)(2,1)} %fusion.29.refs_3_), custom_call_target="tpu_custom_call" | custom-call | tf_op jit(solution)/shard_map/reduce_grads/pallas_call | solution.py:175
  468.0 0.0 slice-start.3
  468.0 0.0 slice-start.4
  468.0 8.4 %copy.22 = f32[3072,768]{1,0:T(8,128)} copy(f32[3072,768]{1,0:T(8,128)} %get-tuple-element.18) | data formatting | bytes 18874368
  476.4 0.0 slice-start.5
  476.4 0.0 slice-start
  476.4 0.0 slice-start.1
  476.4 8.8 %copy.23 = f32[768,3072]{1,0:T(8,128)} copy(f32[768,3072]{1,0:T(8,128)} %get-tuple-element.19) | data formatting | bytes 18874368
  485.1 0.0 slice-done.3
  485.1 0.0 slice-done.4
  485.1 0.0 slice-done.5
  485.1 0.0 slice-start.2
  485.2 3.7 copy.24
  488.9 0.0 slice-done
  488.9 0.0 slice-done.1
  488.9 0.0 slice-done.2
  488.9 3.7 copy.25
  (6 shorter events, 0.0 us)
Async XLA Ops:
  0.6 17.4 %copy-start.2 = (bf16[2048,768]{1,0:T(8,128)(2,1)S(1)}, bf16[2048,768]{1,0:T(8,128)(2,1)}, u32[]{:S(2)}) copy-start(bf16[2048,768]{1,0:T(8,128)(2,1)} %param.13) | copy-start | bytes 9437188
  0.6 17.3 %copy-start = (bf16[2048,3072]{1,0:T(8,128)(2,1)S(1)}, bf16[2048,3072]{1,0:T(8,128)(2,1)}, u32[]{:S(2)}) copy-start(bf16[2048,3072]{1,0:T(8,128)(2,1)} %param.12) | copy-start | bytes 37748740
  0.7 17.3 %copy-start.1 = (bf16[3072,768]{1,0:T(8,128)(2,1)S(1)}, bf16[3072,768]{1,0:T(8,128)(2,1)}, u32[]{:S(2)}) copy-start(bf16[3072,768]{1,0:T(8,128)(2,1)} %param.17) | copy-start | bytes 14155780
  0.7 36.1 %slice-start.9 = ((s8[4718592]{0:T(1024)(128)(4,1)}), s8[4194304]{0:T(1024)(128)(4,1)S(1)}, s32[]{:S(2)}) async-start(s8[4718592]{0:T(1024)(128)(4,1)} %bitcast.24), calls=%async_computation.9 | async-start | bytes 8388608
  18.0 18.8 %slice-start.10 = ((s8[4718592]{0:T(1024)(128)(4,1)}), s8[524288]{0:T(1024)(128)(4,1)S(1)}, s32[]{:S(2)}) async-start(s8[4718592]{0:T(1024)(128)(4,1)} %bitcast.24), calls=%async_computation.10 | async-start | bytes 1048576
  36.8 29.8 %slice-start.6 = ((s8[12582912]{0:T(1024)(128)(4,1)}), s8[4194304]{0:T(1024)(128)(4,1)S(1)}, s32[]{:S(2)}) async-start(s8[12582912]{0:T(1024)(128)(4,1)} %bitcast.22), calls=%async_computation.6 | async-start | bytes 8388608
  36.8 29.8 %slice-start.7 = ((s8[12582912]{0:T(1024)(128)(4,1)}), s8[4194304]{0:T(1024)(128)(4,1)S(1)}, s32[]{:S(2)}) async-start(s8[12582912]{0:T(1024)(128)(4,1)} %bitcast.22), calls=%async_computation.7 | async-start | bytes 8388608
  36.8 45.4 %slice-start.11 = ((s8[4718592]{0:T(1024)(128)(4,1)}), s8[524288]{0:T(1024)(128)(4,1)S(1)}, s32[]{:S(2)}) async-start(s8[4718592]{0:T(1024)(128)(4,1)} %bitcast.26), calls=%async_computation.11 | async-start | bytes 1048576
  51.1 15.5 %slice-start.8 = ((s8[12582912]{0:T(1024)(128)(4,1)}), s8[4194304]{0:T(1024)(128)(4,1)S(1)}, s32[]{:S(2)}) async-start(s8[12582912]{0:T(1024)(128)(4,1)} %bitcast.22), calls=%async_computation.8 | async-start | bytes 8388608
  51.1 31.0 %slice-start.12 = ((s8[4718592]{0:T(1024)(128)(4,1)}), s8[4194304]{0:T(1024)(128)(4,1)S(1)}, s32[]{:S(2)}) async-start(s8[4718592]{0:T(1024)(128)(4,1)} %bitcast.26), calls=%async_computation.12 | async-start | bytes 8388608
  66.6 15.5 %copy-start.4 = (bf16[2048,768]{1,0:T(8,128)(2,1)S(1)}, bf16[2048,768]{1,0:T(8,128)(2,1)}, u32[]{:S(2)}) copy-start(bf16[2048,768]{1,0:T(8,128)(2,1)} %add_convert_fusion.1) | copy-start | bytes 9437188
  66.6 34.1 %slice-start.13 = ((s8[4718592]{0:T(1024)(128)(4,1)}), s8[4194304]{0:T(1024)(128)(4,1)S(1)}, s32[]{:S(2)}) async-start(s8[4718592]{0:T(1024)(128)(4,1)} %bitcast.28), calls=%async_computation.13 | async-start | bytes 8388608
  82.2 18.6 %slice-start.14 = ((s8[4718592]{0:T(1024)(128)(4,1)}), s8[524288]{0:T(1024)(128)(4,1)S(1)}, s32[]{:S(2)}) async-start(s8[4718592]{0:T(1024)(128)(4,1)} %bitcast.28), calls=%async_computation.14 | async-start | bytes 1048576
  100.7 14.7 %copy-start.3 = (bf16[2048,768]{1,0:T(8,128)(2,1)S(1)}, bf16[2048,768]{1,0:T(8,128)(2,1)}, u32[]{:S(2)}) copy-start(bf16[2048,768]{1,0:T(8,128)(2,1)} %param.9) | copy-start | bytes 9437188
  468.0 17.1 %slice-start.3 = ((s8[9437184]{0:T(1024)(128)(4,1)}), s8[4194304]{0:T(1024)(128)(4,1)S(1)}, s32[]{:S(2)}) async-start(s8[9437184]{0:T(1024)(128)(4,1)} %bitcast.20), calls=%async_computation.3 | async-start | bytes 8388608
  468.0 17.1 %slice-start.4 = ((s8[9437184]{0:T(1024)(128)(4,1)}), s8[4194304]{0:T(1024)(128)(4,1)S(1)}, s32[]{:S(2)}) async-start(s8[9437184]{0:T(1024)(128)(4,1)} %bitcast.20), calls=%async_computation.4 | async-start | bytes 8388608
  476.4 8.8 %slice-start.5 = ((s8[9437184]{0:T(1024)(128)(4,1)}), s8[1048576]{0:T(1024)(128)(4,1)S(1)}, s32[]{:S(2)}) async-start(s8[9437184]{0:T(1024)(128)(4,1)} %bitcast.20), calls=%async_computation.5 | async-start | bytes 2097152
  476.4 12.5 %slice-start = ((s8[9437184]{0:T(1024)(128)(4,1)}), s8[4194304]{0:T(1024)(128)(4,1)S(1)}, s32[]{:S(2)}) async-start(s8[9437184]{0:T(1024)(128)(4,1)} %bitcast.18), calls=%async_computation | async-start | bytes 8388608
  476.4 12.5 %slice-start.1 = ((s8[9437184]{0:T(1024)(128)(4,1)}), s8[4194304]{0:T(1024)(128)(4,1)S(1)}, s32[]{:S(2)}) async-start(s8[9437184]{0:T(1024)(128)(4,1)} %bitcast.18), calls=%async_computation.1 | async-start | bytes 8388608
  485.1 3.8 slice-start.2

commit v3 on v1

v3 whole, which is shorter than its diff:
```python
import functools
import heapq
import math
import jax
import jax.numpy as jnp
from jax import lax
from jax.experimental import pallas as pl
from jax.experimental.pallas import tpu as pltpu
from jax.sharding import PartitionSpec as P

AXES = ('third', 'second', 'group')
INV_ROOT_TWO = math.sqrt(0.5)
INV_ROOT_TWO_PI = 1.0 / math.sqrt(2.0 * math.pi)
CONTRACT_COLS = (((1,), (1,)), ((), ()))
CONTRACT_PLAIN = (((1,), (0,)), ((), ()))
MESH = pl.DeviceIdType.MESH
TILES = 12
PAIRS = TILES
CHUNKS = 2 * PAIRS
RING = 3
STAGES = (('x', 'a', 'y', 'b'), ('y', 'a', 'x', 'b'))
STEP_NS = 7000.0
NS_PER_BYTE = 1.0 / 44.0
HOP_NS = 2500.0
EVENT_NS = 400.0


def colour_of(i):
    return (i // 2 + i) % 2


def event_plan(unit, width):
    free = {'x': 0.0, 'y': 0.0, 'z': 0.0}
    arrive = []
    placed = {}
    tail = []

    def run(now, i, stage):
        now += EVENT_NS
        if stage < 8:
            level = stage if stage < 4 else 7 - stage
            axis = STAGES[colour_of(i)][level]
            link = 'z' if axis in 'ab' else axis
            size = (unit >> (level + 1)) * width * 4
            free[link] = max(free[link], now) + size * NS_PER_BYTE
            heapq.heappush(arrive, (free[link] + HOP_NS, i, stage + 1))
        return now

    now = 0.0
    for step in range(2 * TILES):
        for point in range(2):
            now += STEP_NS / 2
            events = []
            if point == 0 and step % 2 == 0 and step >= 2:
                events += [(step - 2, 0), (step - 1, 0)]
            while arrive and arrive[0][0] <= now:
                events.append(heapq.heappop(arrive)[1:])
            for i, stage in events:
                now = run(now, i, stage)
            placed[step, point] = events
    heapq.heappush(arrive, (now + 1000.0, CHUNKS - 2, 0))
    heapq.heappush(arrive, (now + 1000.0, CHUNKS - 1, 0))
    while arrive:
        when, i, stage = heapq.heappop(arrive)
        now = run(max(now, when), i, stage)
        tail.append((i, stage))
    return placed, tail


def step_kernel(*refs):
    x_two, z_two, grad_out, w2_in, w2_out, x_one, z_one, w1_in, w1_out = refs[:9]
    outs, dx_out = refs[9:13], refs[13]
    (acc, rec0, rec1, rec2, rec3, rec_d, tiles, dy, xv, dx_acc, zbuf, wo, wi, ht, dzt,
     send_sem, recv_sem, out_sem, load_sem, dy_sem, x_sem, dx_sem, free_sem, free_d) = refs[14:]
    recs = (rec0, rec1, rec2, rec3)
    unit, width = acc.shape[1], acc.shape[2]
    tokens = dy.shape[0]
    rows_block = min(256, tokens)
    placed, tail = event_plan(unit, width)
    group, second, third = lax.axis_index('group'), lax.axis_index('second'), lax.axis_index('third')
    core = group % 2
    peers = {
        'd': {'group': group + 1 - 2 * core},
        'x': {'group': (group + 2) % 4},
        'y': {'second': 1 - second},
        'a': {'third': third + 1 - 2 * (third % 2)},
        'b': {'third': (third + 2) % 4},
    }
    bits = {'x': group // 2, 'y': second, 'a': third % 2, 'b': third // 2}

    def loads(block, tile, slot):
        z_ref, wo_ref, wi_ref = ((z_two, w2_out, w2_in), (z_one, w1_out, w1_in))[block]
        span = pl.ds(pl.multiple_of(tile * unit, 128), unit)
        return (
            pltpu.make_async_copy(z_ref.at[:, span], zbuf.at[slot], load_sem.at[slot, 0]),
            pltpu.make_async_copy(wo_ref.at[span, :], wo.at[slot], load_sem.at[slot, 1]),
            pltpu.make_async_copy(wi_ref.at[:, span], wi.at[slot], load_sem.at[slot, 2]),
        )

    dy_load = pltpu.make_async_copy(grad_out, dy, dy_sem)
    dy_load.start()
    for copy in loads(0, 0, 0):
        copy.start()
    pltpu.make_async_copy(x_two, xv, x_sem).start()

    barrier = pltpu.get_barrier_semaphore()
    for peer in peers.values():
        pl.semaphore_signal(barrier, inc=1, device_id=peer, device_id_type=MESH)
    pl.semaphore_wait(barrier, len(peers))

    def remote(src, dst, i, k, axis):
        return pltpu.make_async_remote_copy(
            src_ref=src, dst_ref=dst, send_sem=send_sem.at[i, k], recv_sem=recv_sem.at[i, k],
            device_id=peers[axis], device_id_type=MESH)

    def offsets(c):
        offs = [0]
        for k in range(4):
            offs.append(offs[-1] + bits[STAGES[c][k]] * (unit >> (k + 1)))
        return offs

    offs_of = (offsets(0), offsets(1))

    def rows_loop(count, fn):
        block = math.gcd(count, 16)

        @pl.loop(0, count // block)
        def _(t):
            fn(pl.multiple_of(t * block, 8), block)

    def pair_copy(q, kind, i):
        slot = q % RING
        return remote(tiles.at[slot, kind, 1 - core], rec_d.at[slot, kind], i, 0, 'd')

    def out_copies(i):
        block, q, kind = i // TILES, (i // 2) % (TILES // 2), i % 2
        dst = outs[2 * block + kind].at[pl.ds(pl.multiple_of((2 * q + core) * unit, 16), unit), :]
        return remote(acc.at[i], dst, i, 9, 'd'), pltpu.make_async_copy(acc.at[i], dst, out_sem.at[i])

    def level_copy(i, stage):
        axes, offs = STAGES[colour_of(i)], offs_of[colour_of(i)]
        if stage < 4:
            half = unit >> (stage + 1)
            other = pl.multiple_of(offs[stage] + (1 - bits[axes[stage]]) * half, 8)
            return remote(acc.at[i, pl.ds(other, half), :], recs[stage].at[i], i, stage + 1, axes[stage])
        level = 7 - stage
        rows = pl.ds(pl.multiple_of(offs[level + 1], 8), unit >> (level + 1))
        return remote(acc.at[i, rows, :], acc.at[i, rows, :], i, stage + 1, axes[level])

    def event(i, stage):
        axes, offs = STAGES[colour_of(i)], offs_of[colour_of(i)]
        if stage == 0:
            q, kind = i // 2, i % 2
            slot = q % RING
            got = pair_copy(q, kind, i)
            got.wait_recv()

            def first(base):
                def fn(r, block):
                    rows = pl.ds(pl.multiple_of(base + r, 8), block)
                    acc[i, rows, :] = tiles[slot, kind, core, rows, :].astype(jnp.float32) + rec_d[slot, kind, rows, :].astype(jnp.float32)
                return fn

            bit = bits[axes[0]]
            rows_loop(unit // 2, first((1 - bit) * (unit // 2)))
            level_copy(i, 0).start()
            rows_loop(unit // 2, first(bit * (unit // 2)))
            got.wait_send()
            if i + 2 * RING < CHUNKS:
                pl.semaphore_signal(free_d.at[i], inc=1, device_id=peers['d'], device_id_type=MESH)
            return
        arrived = level_copy(i, stage - 1)
        arrived.wait_recv()
        if stage <= 4:
            keep = offs[stage]

            def add(r, block):
                rows = pl.ds(pl.multiple_of(keep + r, 8), block)
                acc[i, rows, :] += recs[stage - 1][i, pl.ds(r, block), :]

            rows_loop(unit >> stage, add)
        if 4 <= stage < 8:
            if stage == 4:
                arrived.wait_send()
                pl.semaphore_signal(free_sem.at[i, 3], inc=1, device_id=peers[axes[3]], device_id_type=MESH)
            pl.semaphore_wait(free_sem.at[i, 7 - stage], 1)
            level_copy(i, stage).start()
        elif stage < 4:
            level_copy(i, stage).start()
            arrived.wait_send()
            pl.semaphore_signal(free_sem.at[i, stage - 1], inc=1, device_id=peers[axes[stage - 1]], device_id_type=MESH)
        else:
            for copy in out_copies(i):
                copy.start()

    def run_events(step, point):
        span = 4
        for lo in range(0, 2 * TILES, span):
            if any(placed[k, point] for k in range(lo, lo + span)):
                @pl.when((step >= lo) & (step < lo + span))
                def _(lo=lo):
                    for k in range(lo, lo + span):
                        if placed[k, point]:
                            @pl.when(step == k)
                            def _(k=k):
                                for i, stage in placed[k, point]:
                                    event(i, stage)

    dy_load.wait()

    @pl.loop(0, tokens // rows_block)
    def _(r):
        rows = pl.ds(pl.multiple_of(r * rows_block, 16), rows_block)
        dx_acc[rows, :] = dy[rows, :].astype(jnp.float32)

    @pl.loop(0, 2 * TILES)
    def _(step):
        slot = step % 2
        for copy in loads(0, 0, slot):
            copy.wait()

        @pl.when(step < TILES - 1)
        def _():
            for copy in loads(0, step + 1, 1 - slot):
                copy.start()

        @pl.when((step >= TILES - 1) & (step < 2 * TILES - 1))
        def _():
            for copy in loads(1, step + 1 - TILES, 1 - slot):
                copy.start()

        @pl.loop(0, tokens // rows_block)
        def _(r):
            rows = pl.ds(pl.multiple_of(r * rows_block, 128), rows_block)
            z_val = zbuf[slot, rows, :].astype(jnp.float32)
            cdf_val = 0.5 * (1.0 + lax.erf(z_val * INV_ROOT_TWO))
            ht[:, rows] = (z_val * cdf_val).astype(jnp.bfloat16).T
            slope = cdf_val + z_val * jnp.exp(-0.5 * z_val * z_val) * INV_ROOT_TWO_PI
            grad_hidden = lax.dot_general(dy[rows, :], wo[slot], CONTRACT_COLS, preferred_element_type=jnp.float32)
            grad_pre = (grad_hidden * slope).astype(jnp.bfloat16)
            dzt[:, rows] = grad_pre.T
            dx_acc[rows, :] += lax.dot_general(grad_pre, wi[slot], CONTRACT_COLS, preferred_element_type=jnp.float32)

        run_events(step, 0)

        @pl.when((step == 0) | (step == TILES))
        def _():
            pltpu.make_async_copy(x_two, xv, x_sem).wait()

        pair = (step // 2) % RING
        tiles[pair, 0, slot] = lax.dot_general(ht[...], dy[...], CONTRACT_PLAIN, preferred_element_type=jnp.float32).astype(jnp.bfloat16)
        tiles[pair, 1, slot] = lax.dot_general(dzt[...], xv[...], CONTRACT_PLAIN, preferred_element_type=jnp.float32).astype(jnp.bfloat16)

        @pl.when((step == TILES - 1) | (step == 2 * TILES - 1))
        def _():
            @pl.loop(0, tokens // rows_block)
            def _(r):
                rows = pl.ds(pl.multiple_of(r * rows_block, 16), rows_block)
                grad_x = dx_acc[rows, :].astype(jnp.bfloat16)
                dy[rows, :] = grad_x
                dx_acc[rows, :] = grad_x.astype(jnp.float32)

        @pl.when(step == TILES - 1)
        def _():
            pltpu.make_async_copy(x_one, xv, x_sem).start()

        @pl.when(slot == 1)
        def _():
            q = step // 2
            for kind in range(2):
                i = 2 * q + kind

                @pl.when(q >= RING)
                def _():
                    pl.semaphore_wait(free_d.at[i - 2 * RING], 1)

                pair_copy(q, kind, i).start()

        run_events(step, 1)

    dx_store = pltpu.make_async_copy(dy, dx_out, dx_sem)
    dx_store.start()
    for i, stage in tail:
        event(i, stage)
    dx_store.wait()
    for i in range(CHUNKS):
        for stage in range(4, 8):
            level_copy(i, stage).wait_send()
        far, near = out_copies(i)
        far.wait()
        near.wait()


def backward_and_reduce(x_one, z_one, x_two, z_two, grad_out, w1_in, w1_out, w2_in, w2_out):
    tokens, width = x_one.shape
    hidden = z_one.shape[1]
    unit = hidden // TILES
    any_spec = pl.BlockSpec(memory_space=pl.ANY)
    bf16, f32 = jnp.bfloat16, jnp.float32
    return pl.pallas_call(
        step_kernel,
        name='backward_and_reduce',
        out_shape=[jax.ShapeDtypeStruct((hidden, width), f32)] * 4 + [jax.ShapeDtypeStruct((tokens, width), bf16)],
        in_specs=[any_spec] * 9,
        out_specs=[any_spec] * 5,
        scratch_shapes=[
            pltpu.VMEM((CHUNKS, unit, width), f32),
            pltpu.VMEM((CHUNKS, unit // 2, width), f32),
            pltpu.VMEM((CHUNKS, unit // 4, width), f32),
            pltpu.VMEM((CHUNKS, unit // 8, width), f32),
            pltpu.VMEM((CHUNKS, unit // 16, width), f32),
            pltpu.VMEM((RING, 2, unit, width), bf16),
            pltpu.VMEM((RING, 2, 2, unit, width), bf16),
            pltpu.VMEM((tokens, width), bf16),
            pltpu.VMEM((tokens, width), bf16),
            pltpu.VMEM((tokens, width), f32),
            pltpu.VMEM((2, tokens, unit), bf16),
            pltpu.VMEM((2, unit, width), bf16),
            pltpu.VMEM((2, width, unit), bf16),
            pltpu.VMEM((unit, tokens), bf16),
            pltpu.VMEM((unit, tokens), bf16),
            pltpu.SemaphoreType.DMA((CHUNKS, 10)),
            pltpu.SemaphoreType.DMA((CHUNKS, 10)),
            pltpu.SemaphoreType.DMA((CHUNKS,)),
            pltpu.SemaphoreType.DMA((2, 3)),
            pltpu.SemaphoreType.DMA,
            pltpu.SemaphoreType.DMA,
            pltpu.SemaphoreType.DMA,
            pltpu.SemaphoreType.REGULAR((CHUNKS, 4)),
            pltpu.SemaphoreType.REGULAR((CHUNKS,)),
        ],
        compiler_params=pltpu.CompilerParams(
            collective_id=0, has_side_effects=True, vmem_limit_bytes=67043328),
    )(x_two, z_two, grad_out, w2_in, w2_out, x_one, z_one, w1_in, w1_out)


def solution(mesh):
    def device_step(*args):
        w2o, w2i_t, w1o, w1i_t, dx_one = backward_and_reduce(*args)
        return w2o, w2i_t.T, w1o, w1i_t.T, dx_one

    row_spec = P(AXES, None)
    repl_spec = P()
    return jax.shard_map(
        device_step,
        mesh=mesh,
        in_specs=(row_spec, row_spec, row_spec, row_spec, row_spec, repl_spec, repl_spec, repl_spec, repl_spec),
        out_specs=(repl_spec, repl_spec, repl_spec, repl_spec, row_spec),
        check_vma=False,
    )
```

time: 1030 us -> 370 us (0.36)
  waiting for transfers between devices: 825 us -> 0 us
  Pallas kernels: 0 us -> 332 us
  matrix products: 141 us -> 0 us
  between operations: 14.2 us -> 0.65 us
  local copies, waits for them, and re-layouts: 48.1 us -> 37 us
    reduce_scatter x4 -> x0, waiting for transfers between devices: 508 us -> none  [reduce_grad(): lax.psum_scatter(grad.astype(jnp.float32), AXES, scatter_dimension=0, til...]
    pallas_call x0 -> x1, Pallas kernels: none -> 332 us  [backward_and_reduce(): pl.pallas_call(step_kernel, name='backward_and_reduce', out_shape=[jax.Sh...]
    all_gather x4 -> x0, waiting for transfers between devices: 317 us -> none  [reduce_grad(): return lax.all_gather(part_sum, AXES, axis=0, tiled=True)]
    dot_general x8 -> x0, matrix products: 141 us -> none  [the longest x2 47 us: block_backward(): lax.dot_general(grad_y, w_out, CONTRACT_COLS, preferred_element_type=jnp....]
    unnamed x28 -> x7, local copies, waits for them, and re-layouts: 48.1 us -> 37 us
  transfers between devices with their start and end apart: 8 -> 0, of which waited for: 8 -> 0; matrix products, arithmetic and copies ran while one was open for 7% -> 0% of each run, Pallas kernels for 0% -> 0%
where the time goes in v3:
time: 370 us
  Pallas kernels  332 us (90%)
  local copies, waits for them, and re-layouts  37 us (10%)
    pallas_call x1, Pallas kernels, backward_and_reduce(): pl.pallas_call(step_kernel, name='backward_and_reduce', out_shape=[jax.Sh...  332 us
    unnamed x7, local copies, waits for them, and re-layouts  37 us

profile of v3, /device:TPU:0, one launch (start us, length us, event | category | flops | bytes accessed | tf_op | source)
XLA Modules:
  0.0 369.6 jit_solution(12311459649591533521)
XLA Ops:
  0.6 331.9 %backward_and_reduce.1 = (f32[3072,768]{1,0:T(8,128)}, f32[3072,768]{1,0:T(8,128)}, f32[3072,768]{1,0:T(8,128)}, f32[3072,768]{1,0:T(8,128)}, bf16[2048,768]{1,0:T(8,128)(2,1)}) custom-call(bf16[2048,768]{1,0:T(8,128)(2,1)} %refs_0_.1, bf16[2048,3072]{1,0:T(8,128)(2,1)} %refs_1_.1, bf16[2048,768]{1,0:T(8,128)(2,1)} %refs_2_.1, bf16[768,3072]{1,0:T(8,128)(2,1)} %refs_3_.1, ...), custom_call_target="tpu_custom_call" | custom-call | tf_op jit(solution)/shard_map/backward_and_reduce/pallas_call | solution.py:300
  332.5 9.6 %copy.14 = f32[768,3072]{1,0:T(8,128)} copy(f32[768,3072]{0,1:T(8,128)} %bitcast.3) | data formatting | bytes 18874368
  342.1 9.6 %copy.15 = f32[768,3072]{1,0:T(8,128)} copy(f32[768,3072]{0,1:T(8,128)} %bitcast.2) | data formatting | bytes 18874368
  351.7 8.0 %copy.19 = f32[3072,768]{1,0:T(8,128)} copy(f32[3072,768]{1,0:T(8,128)} %get-tuple-element.25) | data formatting | bytes 18874368
  359.7 0.0 copy-start
  359.7 8.2 %copy.20 = f32[3072,768]{1,0:T(8,128)} copy(f32[3072,768]{1,0:T(8,128)} %get-tuple-element.27) | data formatting | bytes 18874368
  367.9 0.0 copy-done
  367.9 1.7 copy.21
Async XLA Ops:
  359.7 8.2 %copy-start = (bf16[2048,768]{1,0:T(8,128)(2,1)S(1)}, bf16[2048,768]{1,0:T(8,128)(2,1)}, u32[]{:S(2)}) copy-start(bf16[2048,768]{1,0:T(8,128)(2,1)} %get-tuple-element.29) | copy-start | bytes 9437188

commit v4 on v3

v4 whole, which is shorter than its diff:
```python
import functools
import heapq
import math
import jax
import jax.numpy as jnp
from jax import lax
from jax.experimental import pallas as pl
from jax.experimental.pallas import tpu as pltpu
from jax.sharding import PartitionSpec as P

AXES = ('third', 'second', 'group')
INV_ROOT_TWO = math.sqrt(0.5)
INV_ROOT_TWO_PI = 1.0 / math.sqrt(2.0 * math.pi)
CONTRACT_COLS = (((1,), (1,)), ((), ()))
CONTRACT_PLAIN = (((1,), (0,)), ((), ()))
MESH = pl.DeviceIdType.MESH
TILES = 12
PAIRS = TILES
CHUNKS = 2 * PAIRS
RING = 3
STEP_NS = 5500.0
NS_PER_BYTE = 1.0 / 45.0
HOP_NS = 2200.0
EVENT_NS = 300.0
POINTS = 2


def event_plan(unit, width):
    free = {}
    arrive = []
    placed = {}
    tail = []
    row = width * 4 * NS_PER_BYTE
    quarter = unit // 8

    def run(now, q, stage):
        now += EVENT_NS
        if stage == 0 or stage == 9:
            sends = [('plane', unit // 2)]
        elif stage <= 3:
            sends = [(stage, 2 * (4 - stage) * quarter)]
        elif stage <= 5:
            sends = [('plane', quarter // 2)]
        elif stage <= 8:
            sends = [(k, 2 * quarter) for k in range(stage - 5, 4)]
        else:
            return now
        for link, rows in sends:
            free[link] = max(free.get(link, 0.0), now) + rows * row
        heapq.heappush(arrive, (max(free[link] for link, _ in sends) + HOP_NS, q, stage + 1))
        return now

    now = 0.0
    for step in range(2 * TILES):
        for point in range(POINTS):
            now += STEP_NS / POINTS
            events = []
            if point == 0 and step % 2 == 0 and step >= 2:
                events.append((step // 2 - 1, 0))
            while arrive and arrive[0][0] <= now:
                events.append(heapq.heappop(arrive)[1:])
            for q, stage in events:
                now = run(now, q, stage)
            placed[step, point] = events
    heapq.heappush(arrive, (now + 1000.0, PAIRS - 1, 0))
    while arrive:
        when, q, stage = heapq.heappop(arrive)
        now = run(max(now, when), q, stage)
        tail.append((q, stage))
    return placed, tail


def step_kernel(*refs):
    x_two, z_two, grad_out, w2_in, w2_out, x_one, z_one, w1_in, w1_out = refs[:9]
    outs, dx_out = refs[9:13], refs[13]
    (acc, rec_first, rec_line, rec_last, rec_d, tiles, dy, xv, dx_acc, zbuf, wo, wi, ht, dzt,
     send_sem, recv_sem, out_sem, load_sem, dy_sem, x_sem, dx_sem, free_sem, free_line, free_d) = refs[14:]
    unit, width = acc.shape[1], acc.shape[2]
    tokens = dy.shape[0]
    rows_block = min(256, tokens)
    placed, tail = event_plan(unit, width)
    group, second, third = lax.axis_index('group'), lax.axis_index('second'), lax.axis_index('third')
    core, x_bit = lax.rem(group, 2), group // 2
    half, quarter, piece = unit // 2, unit // 8, unit // 16
    peer_core = {'group': group + 1 - 2 * core}
    peer_x = {'group': group + 2 - 4 * x_bit}
    peer_y = {'second': 1 - second}
    peer_up, peer_down = {'third': lax.rem(third + 1, 4)}, {'third': lax.rem(third + 3, 4)}
    at = [third == place for place in range(4)]
    above, below = [third >= hop for hop in range(4)], [third <= 3 - hop for hop in range(4)]
    can_up, can_down = below[1], above[1]
    turn = [lax.rem(third + c, 4) * quarter for c in range(4)]

    def loads(block, tile, slot):
        z_ref, wo_ref, wi_ref = ((z_two, w2_out, w2_in), (z_one, w1_out, w1_in))[block]
        span = pl.ds(pl.multiple_of(tile * unit, 128), unit)
        return (
            pltpu.make_async_copy(z_ref.at[:, span], zbuf.at[slot], load_sem.at[slot, 0]),
            pltpu.make_async_copy(wo_ref.at[span, :], wo.at[slot], load_sem.at[slot, 1]),
            pltpu.make_async_copy(wi_ref.at[:, span], wi.at[slot], load_sem.at[slot, 2]),
        )

    dy_load = pltpu.make_async_copy(grad_out, dy, dy_sem)
    dy_load.start()
    for copy in loads(0, 0, 0):
        copy.start()
    pltpu.make_async_copy(x_two, xv, x_sem).start()

    barrier = pltpu.get_barrier_semaphore()
    for peer in (peer_core, peer_x, peer_y, peer_up, peer_down):
        pl.semaphore_signal(barrier, inc=1, device_id=peer, device_id_type=MESH)
    pl.semaphore_wait(barrier, 5)

    def remote(src, dst, i, k, peer):
        return pltpu.make_async_remote_copy(
            src_ref=src, dst_ref=dst, send_sem=send_sem.at[i, k], recv_sem=recv_sem.at[i, k],
            device_id=peer, device_id_type=MESH)

    def rows_loop(count, fn):
        block = math.gcd(count, 16)

        @pl.loop(0, count // block)
        def _(t):
            fn(pl.multiple_of(t * block, 8), block)

    def pair_copy(q, kind, i):
        slot = q % RING
        return remote(tiles.at[slot, kind, 1 - core], rec_d.at[slot, kind], i, 0, peer_core)

    def out_copies(i, kind, tile):
        block = tile // TILES
        out = outs[2 * block + kind]
        span = pl.ds(pl.multiple_of((tile - TILES * block + core) * unit, 128), unit)
        copies = []
        if kind == 0:
            pairs = [(acc.at[i], out.at[span, :])]
        else:
            pairs = [(acc.at[i, :, pl.ds(b * unit, unit)], out.at[pl.ds(b * unit, unit), span]) for b in range(width // unit)]
        for b, (src, dst) in enumerate(pairs):
            copies += [remote(src, dst, i, 13 + b, peer_core), pltpu.make_async_copy(src, dst, out_sem.at[i, b])]
        return copies

    class Chunk:
        def __init__(self, q, kind):
            self.q, self.kind, self.i = q, kind, 2 * q + kind
            colour = lax.rem(q + kind, 2)
            self.first_bit = x_bit + colour * (second - x_bit)
            self.last_bit = second + colour * (x_bit - second)
            self.first_peer = {'group': group + (1 - colour) * (2 - 4 * x_bit), 'second': second + colour * (1 - 2 * second)}
            self.last_peer = {'group': group + colour * (2 - 4 * x_bit), 'second': second + (1 - colour) * (1 - 2 * second)}
            self.kept = pl.multiple_of(self.first_bit * half, 8)
            self.other = pl.multiple_of(half - self.kept, 8)

        def span(self, row, count):
            return acc.at[self.i, pl.ds(pl.multiple_of(row, 8), count), :]

        def first(self):
            slot = 2 * (self.q % (PAIRS // 2)) + self.kind
            return remote(self.span(self.other, half), rec_first.at[slot], self.i, 1, self.first_peer)

        def up(self, place):
            rows = (3 - place) * quarter
            return remote(self.span(self.kept + (place + 1) * quarter, rows), rec_line.at[self.i, pl.ds(0, rows), :], self.i, 2, peer_up)

        def down(self, place):
            rows = place * quarter
            dst = rec_line.at[self.i, pl.ds((5 - place) * quarter, rows), :]
            return remote(self.span(self.kept, rows), dst, self.i, 3, peer_down)

        def mine(self):
            return self.kept + turn[0] + self.last_bit * piece

        def last(self):
            other = self.kept + turn[0] + (1 - self.last_bit) * piece
            return remote(self.span(other, piece), rec_last.at[self.i], self.i, 4, self.last_peer)

        def last_back(self):
            ref = self.span(self.mine(), piece)
            return remote(ref, ref, self.i, 5, self.last_peer)

        def spread_up(self, hop, arriving=0):
            ref = self.span(self.kept + turn[(5 - hop - arriving) % 4], quarter)
            return remote(ref, ref, self.i, 5 + hop, peer_up)

        def spread_down(self, hop, arriving=0):
            ref = self.span(self.kept + turn[(hop - 1 + arriving) % 4], quarter)
            return remote(ref, ref, self.i, 8 + hop, peer_down)

        def first_back(self):
            ref = self.span(self.kept, half)
            return remote(ref, ref, self.i, 12, self.first_peer)

    def signal(sem, peer):
        pl.semaphore_signal(sem, inc=1, device_id=peer, device_id_type=MESH)

    def add_rows(i, base, rec, rec_index, rec_base, count):
        def add(r, block):
            rows = pl.ds(pl.multiple_of(base + r, 8), block)
            acc[i, rows, :] += rec[rec_index, pl.ds(pl.multiple_of(rec_base + r, 8), block), :]

        rows_loop(count, add)

    def chunk_event(q, kind, stage):
        chunk = Chunk(q, kind)
        i, kept = chunk.i, chunk.kept
        if stage == 0:
            slot = q % RING
            got = pair_copy(q, kind, i)
            got.wait_recv()

            def first(base):
                def fn(r, block):
                    rows = pl.ds(pl.multiple_of(base + r, 8), block)
                    acc[i, rows, :] = tiles[slot, kind, core, rows, :].astype(jnp.float32) + rec_d[slot, kind, rows, :].astype(jnp.float32)
                return fn

            rows_loop(half, first(chunk.other))
            if q >= PAIRS // 2:
                pl.semaphore_wait(free_sem.at[i - PAIRS, 2], 1)
            chunk.first().start()
            rows_loop(half, first(kept))
            got.wait_send()
            if q + RING < PAIRS:
                signal(free_d.at[i], peer_core)
        elif stage == 1:
            got = chunk.first()
            got.wait_recv()
            add_rows(i, kept, rec_first, 2 * (q % (PAIRS // 2)) + kind, 0, half)

            @pl.when(at[0])
            def _():
                chunk.up(0).start()

            @pl.when(at[3])
            def _():
                chunk.down(3).start()

            if q < PAIRS // 2:
                signal(free_sem.at[i, 2], chunk.first_peer)
            got.wait_send()
            signal(free_sem.at[i, 0], chunk.first_peer)
        elif stage <= 4:
            hop = stage - 1

            @pl.when(at[hop])
            def _():
                chunk.up(hop - 1).wait_recv()
                add_rows(i, kept + hop * quarter, rec_line, i, 0, (4 - hop) * quarter)
                if hop < 3:
                    chunk.up(hop).start()

            @pl.when(at[3 - hop])
            def _():
                chunk.down(4 - hop).wait_recv()
                add_rows(i, kept, rec_line, i, (1 + hop) * quarter, (4 - hop) * quarter)
                if hop < 3:
                    chunk.down(3 - hop).start()

            if hop == 3:
                chunk.last().start()
        elif stage == 5:
            got = chunk.last()
            got.wait_recv()
            add_rows(i, chunk.mine(), rec_last, i, 0, piece)
            got.wait_send()
            signal(free_sem.at[i, 1], chunk.last_peer)
            pl.semaphore_wait(free_sem.at[i, 1], 1)
            chunk.last_back().start()
            for place in range(4):
                @pl.when(at[place])
                def _(place=place):
                    if place < 3:
                        chunk.up(place).wait_send()
                        signal(free_line.at[i, 0], peer_up)
                    if place > 0:
                        chunk.down(place).wait_send()
                        signal(free_line.at[i, 1], peer_down)
        elif stage == 6:
            chunk.last_back().wait_recv()

            @pl.when(can_up)
            def _():
                pl.semaphore_wait(free_line.at[i, 1], 1)
                chunk.spread_up(1).start()

            @pl.when(can_down)
            def _():
                pl.semaphore_wait(free_line.at[i, 0], 1)
                chunk.spread_down(1).start()
        elif stage <= 9:
            hop = stage - 6

            @pl.when(above[hop])
            def _():
                chunk.spread_up(hop, 1).wait_recv()
                if hop < 3:
                    @pl.when(can_up)
                    def _():
                        chunk.spread_up(hop + 1).start()

            @pl.when(below[hop])
            def _():
                chunk.spread_down(hop, 1).wait_recv()
                if hop < 3:
                    @pl.when(can_down)
                    def _():
                        chunk.spread_down(hop + 1).start()

            if hop == 3:
                pl.semaphore_wait(free_sem.at[i, 0], 1)
                chunk.first_back().start()
        else:
            chunk.first_back().wait_recv()

    def event(q, stage):
        @pl.loop(0, 2)
        def _(kind):
            chunk_event(q, kind, stage)

        if stage == 10:
            for kind in range(2):
                for copy in out_copies(2 * q + kind, kind, 2 * q):
                    copy.start()

    def run_events(step, point):
        span = 4
        for lo in range(0, 2 * TILES, span):
            if any(placed[k, point] for k in range(lo, lo + span)):
                @pl.when((step >= lo) & (step < lo + span))
                def _(lo=lo):
                    for k in range(lo, lo + span):
                        if placed[k, point]:
                            @pl.when(step == k)
                            def _(k=k):
                                for q, stage in placed[k, point]:
                                    event(q, stage)

    dy_load.wait()

    @pl.loop(0, tokens // rows_block)
    def _(r):
        rows = pl.ds(pl.multiple_of(r * rows_block, 16), rows_block)
        dx_acc[rows, :] = dy[rows, :].astype(jnp.float32)

    @pl.loop(0, 2 * TILES)
    def _(step):
        slot = step % 2
        for copy in loads(0, 0, slot):
            copy.wait()

        @pl.when(step < TILES - 1)
        def _():
            for copy in loads(0, step + 1, 1 - slot):
                copy.start()

        @pl.when((step >= TILES - 1) & (step < 2 * TILES - 1))
        def _():
            for copy in loads(1, step + 1 - TILES, 1 - slot):
                copy.start()

        @pl.loop(0, tokens // rows_block)
        def _(r):
            rows = pl.ds(pl.multiple_of(r * rows_block, 128), rows_block)
            z_val = zbuf[slot, rows, :].astype(jnp.float32)
            cdf_val = 0.5 * (1.0 + lax.erf(z_val * INV_ROOT_TWO))
            ht[:, rows] = (z_val * cdf_val).astype(jnp.bfloat16).T
            slope = cdf_val + z_val * jnp.exp(-0.5 * z_val * z_val) * INV_ROOT_TWO_PI
            grad_hidden = lax.dot_general(dy[rows, :], wo[slot], CONTRACT_COLS, preferred_element_type=jnp.float32)
            grad_pre = (grad_hidden * slope).astype(jnp.bfloat16)
            dzt[:, rows] = grad_pre.T
            dx_acc[rows, :] += lax.dot_general(grad_pre, wi[slot], CONTRACT_COLS, preferred_element_type=jnp.float32)

        run_events(step, 0)

        @pl.when((step == 0) | (step == TILES))
        def _():
            pltpu.make_async_copy(x_two, xv, x_sem).wait()

        pair = (step // 2) % RING
        tiles[pair, 0, slot] = lax.dot_general(ht[...], dy[...], CONTRACT_PLAIN, preferred_element_type=jnp.float32).astype(jnp.bfloat16)
        for b in range(width // unit):
            cols = pl.ds(b * unit, unit)
            tile = lax.dot_general(dzt[...], xv[:, cols], CONTRACT_PLAIN, preferred_element_type=jnp.float32)
            tiles[pair, 1, slot, :, cols] = tile.T.astype(jnp.bfloat16)

        @pl.when((step == TILES - 1) | (step == 2 * TILES - 1))
        def _():
            @pl.loop(0, tokens // rows_block)
            def _(r):
                rows = pl.ds(pl.multiple_of(r * rows_block, 16), rows_block)
                grad_x = dx_acc[rows, :].astype(jnp.bfloat16)
                dy[rows, :] = grad_x
                dx_acc[rows, :] = grad_x.astype(jnp.float32)

        @pl.when(step == TILES - 1)
        def _():
            pltpu.make_async_copy(x_one, xv, x_sem).start()

        @pl.when(slot == 1)
        def _():
            q = step // 2
            for kind in range(2):
                i = 2 * q + kind

                @pl.when(q >= RING)
                def _():
                    pl.semaphore_wait(free_d.at[i - 2 * RING], 1)

                pair_copy(q, kind, i).start()

        run_events(step, 1)

    dx_store = pltpu.make_async_copy(dy, dx_out, dx_sem)
    dx_store.start()
    for q, stage in tail:
        event(q, stage)
    dx_store.wait()

    @pl.loop(0, PAIRS)
    def _(q):
        for kind in range(2):
            chunk = Chunk(q, kind)
            chunk.last_back().wait_send()
            for hop in range(1, 4):
                @pl.when(above[hop - 1] & can_up)
                def _(chunk=chunk, hop=hop):
                    chunk.spread_up(hop).wait_send()

                @pl.when(below[hop - 1] & can_down)
                def _(chunk=chunk, hop=hop):
                    chunk.spread_down(hop).wait_send()
            chunk.first_back().wait_send()

    for q in range(PAIRS):
        for kind in range(2):
            for copy in out_copies(2 * q + kind, kind, 2 * q):
                copy.wait()


def backward_and_reduce(x_one, z_one, x_two, z_two, grad_out, w1_in, w1_out, w2_in, w2_out):
    tokens, width = x_one.shape
    hidden = z_one.shape[1]
    unit = hidden // TILES
    any_spec = pl.BlockSpec(memory_space=pl.ANY)
    bf16, f32 = jnp.bfloat16, jnp.float32
    return pl.pallas_call(
        step_kernel,
        name='backward_and_reduce',
        out_shape=[jax.ShapeDtypeStruct((hidden, width), f32), jax.ShapeDtypeStruct((width, hidden), f32)] * 2 + [jax.ShapeDtypeStruct((tokens, width), bf16)],
        in_specs=[any_spec] * 9,
        out_specs=[any_spec] * 5,
        scratch_shapes=[
            pltpu.VMEM((CHUNKS, unit, width), f32),
            pltpu.VMEM((PAIRS, unit // 2, width), f32),
            pltpu.VMEM((CHUNKS, 5 * unit // 8, width), f32),
            pltpu.VMEM((CHUNKS, unit // 16, width), f32),
            pltpu.VMEM((RING, 2, unit, width), bf16),
            pltpu.VMEM((RING, 2, 2, unit, width), bf16),
            pltpu.VMEM((tokens, width), bf16),
            pltpu.VMEM((tokens, width), bf16),
            pltpu.VMEM((tokens, width), f32),
            pltpu.VMEM((2, tokens, unit), bf16),
            pltpu.VMEM((2, unit, width), bf16),
            pltpu.VMEM((2, width, unit), bf16),
            pltpu.VMEM((unit, tokens), bf16),
            pltpu.VMEM((unit, tokens), bf16),
            pltpu.SemaphoreType.DMA((CHUNKS, 13 + width // unit)),
            pltpu.SemaphoreType.DMA((CHUNKS, 13 + width // unit)),
            pltpu.SemaphoreType.DMA((CHUNKS, width // unit)),
            pltpu.SemaphoreType.DMA((2, 3)),
            pltpu.SemaphoreType.DMA,
            pltpu.SemaphoreType.DMA,
            pltpu.SemaphoreType.DMA,
            pltpu.SemaphoreType.REGULAR((CHUNKS, 3)),
            pltpu.SemaphoreType.REGULAR((CHUNKS, 2)),
            pltpu.SemaphoreType.REGULAR((CHUNKS,)),
        ],
        compiler_params=pltpu.CompilerParams(
            collective_id=0, has_side_effects=True, vmem_limit_bytes=67043328),
    )(x_two, z_two, grad_out, w2_in, w2_out, x_one, z_one, w1_in, w1_out)


def solution(mesh):
    def device_step(*args):
        return tuple(backward_and_reduce(*args))

    row_spec = P(AXES, None)
    repl_spec = P()
    return jax.shard_map(
        device_step,
        mesh=mesh,
        in_specs=(row_spec, row_spec, row_spec, row_spec, row_spec, repl_spec, repl_spec, repl_spec, repl_spec),
        out_specs=(repl_spec, repl_spec, repl_spec, repl_spec, row_spec),
        check_vma=False,
    )
```

time: 370 us -> 396 us (1.070)
  Pallas kernels: 332 us -> 369 us
  local copies, waits for them, and re-layouts: 37 us -> 26.8 us
    pallas_call x1, Pallas kernels: 332 us -> 369 us  [backward_and_reduce(): pl.pallas_call(step_kernel, name='backward_and_reduce', out_shape=[jax.Sh...]
    unnamed x7 -> x19, local copies, waits for them, and re-layouts: 37 us -> 26.8 us
where the time goes in v4:
time: 396 us
  Pallas kernels  369 us (93%)
  local copies, waits for them, and re-layouts  26.8 us (7%)
    pallas_call x1, Pallas kernels, backward_and_reduce(): pl.pallas_call(step_kernel, name='backward_and_reduce', out_shape=[jax.Sh...  369 us
    unnamed x19, local copies, waits for them, and re-layouts  26.8 us

profile of v4, /device:TPU:0, one launch (start us, length us, event | category | flops | bytes accessed | tf_op | source)
XLA Modules:
  0.0 396.1 jit_solution(2861937727249985474)
XLA Ops:
  0.6 368.6 %backward_and_reduce.1 = (f32[3072,768]{1,0:T(8,128)}, f32[768,3072]{1,0:T(8,128)}, f32[3072,768]{1,0:T(8,128)}, f32[768,3072]{1,0:T(8,128)}, bf16[2048,768]{1,0:T(8,128)(2,1)}) custom-call(bf16[2048,768]{1,0:T(8,128)(2,1)} %refs_0_.1, bf16[2048,3072]{1,0:T(8,128)(2,1)} %refs_1_.1, bf16[2048,768]{1,0:T(8,128)(2,1)} %refs_2_.1, bf16[768,3072]{1,0:T(8,128)(2,1)} %refs_3_.1, ...), custom_call_target="tpu_custom_call" | custom-call | tf_op jit(solution)/shard_map/backward_and_reduce/pallas_call | solution.py:446
  369.2 0.0 slice-start.3
  369.2 0.0 slice-start.4
  369.2 8.4 %copy.19 = f32[3072,768]{1,0:T(8,128)} copy(f32[3072,768]{1,0:T(8,128)} %get-tuple-element.10) | data formatting | bytes 18874368
  377.6 0.0 slice-start.5
  377.6 0.0 slice-start
  377.6 0.0 slice-start.1
  377.6 8.8 %copy.20 = f32[768,3072]{1,0:T(8,128)} copy(f32[768,3072]{1,0:T(8,128)} %get-tuple-element.11) | data formatting | bytes 18874368
  386.4 0.0 slice-done.3
  386.4 0.0 slice-done.4
  386.4 0.0 slice-done.5
  386.4 0.0 slice-start.2
  386.4 3.7 copy.21
  390.1 0.0 slice-done
  390.1 0.0 slice-done.1
  390.1 0.0 slice-done.2
  390.2 0.0 copy-start
  390.2 4.2 %copy.22 = f32[768,3072]{1,0:T(8,128)} copy(f32[768,3072]{1,0:T(8,128)S(1)} %bitcast.1) | data formatting | bytes 18874368
  394.4 0.0 copy-done
  394.4 1.7 copy.23
  (2 shorter events, 0.0 us)
Async XLA Ops:
  369.2 17.1 %slice-start.3 = ((s8[9437184]{0:T(1024)(128)(4,1)}), s8[4194304]{0:T(1024)(128)(4,1)S(1)}, s32[]{:S(2)}) async-start(s8[9437184]{0:T(1024)(128)(4,1)} %bitcast.2), calls=%async_computation.3 | async-start | bytes 8388608
  369.2 17.1 %slice-start.4 = ((s8[9437184]{0:T(1024)(128)(4,1)}), s8[4194304]{0:T(1024)(128)(4,1)S(1)}, s32[]{:S(2)}) async-start(s8[9437184]{0:T(1024)(128)(4,1)} %bitcast.2), calls=%async_computation.4 | async-start | bytes 8388608
  377.6 8.8 %slice-start.5 = ((s8[9437184]{0:T(1024)(128)(4,1)}), s8[1048576]{0:T(1024)(128)(4,1)S(1)}, s32[]{:S(2)}) async-start(s8[9437184]{0:T(1024)(128)(4,1)} %bitcast.2), calls=%async_computation.5 | async-start | bytes 2097152
  377.6 12.5 %slice-start = ((s8[9437184]{0:T(1024)(128)(4,1)}), s8[4194304]{0:T(1024)(128)(4,1)S(1)}, s32[]{:S(2)}) async-start(s8[9437184]{0:T(1024)(128)(4,1)} %bitcast), calls=%async_computation | async-start | bytes 8388608
  377.6 12.5 %slice-start.1 = ((s8[9437184]{0:T(1024)(128)(4,1)}), s8[4194304]{0:T(1024)(128)(4,1)S(1)}, s32[]{:S(2)}) async-start(s8[9437184]{0:T(1024)(128)(4,1)} %bitcast), calls=%async_computation.1 | async-start | bytes 8388608
  386.4 3.8 slice-start.2
  390.2 4.3 %copy-start = (bf16[2048,768]{1,0:T(8,128)(2,1)S(1)}, bf16[2048,768]{1,0:T(8,128)(2,1)}, u32[]{:S(2)}) copy-start(bf16[2048,768]{1,0:T(8,128)(2,1)} %get-tuple-element.14) | copy-start | bytes 9437188

commit v5 on v4

--- a/solution.py
+++ b/solution.py
@@ -1,5 +1,4 @@
 import functools
-import heapq
 import math
 import jax
 import jax.numpy as jnp
@@ -18,55 +17,31 @@
 PAIRS = TILES
 CHUNKS = 2 * PAIRS
 RING = 3
-STEP_NS = 5500.0
-NS_PER_BYTE = 1.0 / 45.0
-HOP_NS = 2200.0
-EVENT_NS = 300.0
-POINTS = 2
-
-
-def event_plan(unit, width):
-    free = {}
-    arrive = []
-    placed = {}
-    tail = []
-    row = width * 4 * NS_PER_BYTE
-    quarter = unit // 8
-
-    def run(now, q, stage):
-        now += EVENT_NS
-        if stage == 0 or stage == 9:
-            sends = [('plane', unit // 2)]
-        elif stage <= 3:
-            sends = [(stage, 2 * (4 - stage) * quarter)]
-        elif stage <= 5:
-            sends = [('plane', quarter // 2)]
-        elif stage <= 8:
-            sends = [(k, 2 * quarter) for k in range(stage - 5, 4)]
+POINTS = 4
+ORDER = (
+    -1, -1, -1, -1, -1, -1, -1, -1, -1, 0, -1, -1, -1, -1, -1, -1, 1, -1, -1, 11, -1, -1, -1, -1,
+    -1, 2, 12, -1, -1, -1, 22, -1, -1, 3, -1, -1, -1, 4, 13, 23, -1, 5, -1, -1, 33, 6, -1, -1,
+    14, -1, -1, 24, -1, 34, 15, -1, 7, -1, -1, 16, 44, 25, 17, -1, -1, -1, 35, 8, 26, -1, 45, 18,
+    27, -1, 9, -1, 28, -1, -1, 36, 55, 19, -1, 46, -1, -1, -1, 29, 37, 20, -1, 56, 38, 47, -1, -1,
+    -1, 30, 66, -1, 39, -1, 48, -1, 31, 57, -1, -1, 67, 40, -1, -1, 10, 49, 58, 21, 77, -1, 50, -1,
+    41, -1, 68, 59, -1, -1, 51, 78, 60, 42, -1, -1, -1, 32, 69, -1, 88, 52, 61, -1, -1, 79, -1, -1,
+    70, 53, -1, 62, 89, -1, -1, 80, 71, -1, 99, 63, -1, 72, -1, -1, 90, 81, -1, 64, -1, 100, 73, -1,
+    -1, 82, 91, 110, -1, 83, -1, 92, -1, 74, 101, -1, -1, 84, 111, 93, 75, -1, 54, 94, -1, -1, 85, 102,
+    121, 112, 95, 103, 113, 122, 104, 114, 96, 105, 115, 65, 86, 116, 76, 123, 97, 106, 117, 124, 125, 107, 126, 108,
+    127, 87, 118, 128, 119, 129, 130, 98, 43, 109, 120, 131,
+)
+
+
+def event_plan():
+    placed = {(step, point): [] for step in range(2 * TILES) for point in range(POINTS)}
+    quarters, tail = 0, []
+    for entry in ORDER:
+        if entry < 0:
+            quarters += 1
+        elif quarters < 2 * TILES * POINTS:
+            placed[(quarters - 1) // POINTS, (quarters - 1) % POINTS].append(divmod(entry, 11))
         else:
-            return now
-        for link, rows in sends:
-            free[link] = max(free.get(link, 0.0), now) + rows * row
-        heapq.heappush(arrive, (max(free[link] for link, _ in sends) + HOP_NS, q, stage + 1))
-        return now
-
-    now = 0.0
-    for step in range(2 * TILES):
-        for point in range(POINTS):
-            now += STEP_NS / POINTS
-            events = []
-            if point == 0 and step % 2 == 0 and step >= 2:
-                events.append((step // 2 - 1, 0))
-            while arrive and arrive[0][0] <= now:
-                events.append(heapq.heappop(arrive)[1:])
-            for q, stage in events:
-                now = run(now, q, stage)
-            placed[step, point] = events
-    heapq.heappush(arrive, (now + 1000.0, PAIRS - 1, 0))
-    while arrive:
-        when, q, stage = heapq.heappop(arrive)
-        now = run(max(now, when), q, stage)
-        tail.append((q, stage))
+            tail.append(divmod(entry, 11))
     return placed, tail
 
 
@@ -78,7 +53,7 @@
     unit, width = acc.shape[1], acc.shape[2]
     tokens = dy.shape[0]
     rows_block = min(256, tokens)
-    placed, tail = event_plan(unit, width)
+    placed, tail = event_plan()
     group, second, third = lax.axis_index('group'), lax.axis_index('second'), lax.axis_index('third')
     core, x_bit = lax.rem(group, 2), group // 2
     half, quarter, piece = unit // 2, unit // 8, unit // 16
@@ -358,8 +333,7 @@
             for copy in loads(1, step + 1 - TILES, 1 - slot):
                 copy.start()
 
-        @pl.loop(0, tokens // rows_block)
-        def _(r):
+        def token_rows(r):
             rows = pl.ds(pl.multiple_of(r * rows_block, 128), rows_block)
             z_val = zbuf[slot, rows, :].astype(jnp.float32)
             cdf_val = 0.5 * (1.0 + lax.erf(z_val * INV_ROOT_TWO))
@@ -370,14 +344,20 @@
             dzt[:, rows] = grad_pre.T
             dx_acc[rows, :] += lax.dot_general(grad_pre, wi[slot], CONTRACT_COLS, preferred_element_type=jnp.float32)
 
+        split = max(1, tokens // rows_block // 2)
+        pl.loop(0, split)(token_rows)
         run_events(step, 0)
-
-        @pl.when((step == 0) | (step == TILES))
-        def _():
-            pltpu.make_async_copy(x_two, xv, x_sem).wait()
+        pl.loop(split, tokens // rows_block)(token_rows)
+        run_events(step, 1)
 
         pair = (step // 2) % RING
         tiles[pair, 0, slot] = lax.dot_general(ht[...], dy[...], CONTRACT_PLAIN, preferred_element_type=jnp.float32).astype(jnp.bfloat16)
+        run_events(step, 2)
+
+        @pl.when((step == 0) | (step == TILES))
+        def _():
+            pltpu.make_async_copy(x_two, xv, x_sem).wait()
+
         for b in range(width // unit):
             cols = pl.ds(b * unit, unit)
             tile = lax.dot_general(dzt[...], xv[:, cols], CONTRACT_PLAIN, preferred_element_type=jnp.float32)
@@ -408,7 +388,7 @@
 
                 pair_copy(q, kind, i).start()
 
-        run_events(step, 1)
+        run_events(step, 3)
 
     dx_store = pltpu.make_async_copy(dy, dx_out, dx_sem)
     dx_store.start()

time: 396 us -> 353 us (0.89)
  Pallas kernels: 369 us -> 325 us
    pallas_call x1, Pallas kernels: 369 us -> 325 us  [backward_and_reduce(): pl.pallas_call(step_kernel, name='backward_and_reduce', out_shape=[jax.Sh...]
where the time goes in v5:
time: 353 us
  Pallas kernels  325 us (92%)
  local copies, waits for them, and re-layouts  26.8 us (8%)
    pallas_call x1, Pallas kernels, backward_and_reduce(): pl.pallas_call(step_kernel, name='backward_and_reduce', out_shape=[jax.Sh...  325 us
    unnamed x19, local copies, waits for them, and re-layouts  26.8 us

profile of v5, /device:TPU:0, one launch (start us, length us, event | category | flops | bytes accessed | tf_op | source)
XLA Modules:
  0.0 352.6 jit_solution(6756218192010446512)
XLA Ops:
  0.6 325.1 %backward_and_reduce.1 = (f32[3072,768]{1,0:T(8,128)}, f32[768,3072]{1,0:T(8,128)}, f32[3072,768]{1,0:T(8,128)}, f32[768,3072]{1,0:T(8,128)}, bf16[2048,768]{1,0:T(8,128)(2,1)}) custom-call(bf16[2048,768]{1,0:T(8,128)(2,1)} %refs_0_.1, bf16[2048,3072]{1,0:T(8,128)(2,1)} %refs_1_.1, bf16[2048,768]{1,0:T(8,128)(2,1)} %refs_2_.1, bf16[768,3072]{1,0:T(8,128)(2,1)} %refs_3_.1, ...), custom_call_target="tpu_custom_call" | custom-call | tf_op jit(solution)/shard_map/backward_and_reduce/pallas_call | solution.py:426
  325.7 0.0 slice-start.3
  325.8 0.0 slice-start.4
  325.8 8.4 %copy.19 = f32[3072,768]{1,0:T(8,128)} copy(f32[3072,768]{1,0:T(8,128)} %get-tuple-element.10) | data formatting | bytes 18874368
  334.1 0.0 slice-start.5
  334.1 0.0 slice-start
  334.1 0.0 slice-start.1
  334.1 8.8 %copy.20 = f32[768,3072]{1,0:T(8,128)} copy(f32[768,3072]{1,0:T(8,128)} %get-tuple-element.11) | data formatting | bytes 18874368
  342.9 0.0 slice-done.3
  342.9 0.0 slice-done.4
  342.9 0.0 slice-done.5
  342.9 0.0 slice-start.2
  342.9 3.7 %copy.21 = f32[3072,768]{1,0:T(8,128)} copy(f32[3072,768]{1,0:T(8,128)S(1)} %bitcast.3) | data formatting | bytes 18874368
  346.7 0.0 slice-done
  346.7 0.0 slice-done.1
  346.7 0.0 slice-done.2
  346.7 0.0 copy-start
  346.7 4.2 %copy.22 = f32[768,3072]{1,0:T(8,128)} copy(f32[768,3072]{1,0:T(8,128)S(1)} %bitcast.1) | data formatting | bytes 18874368
  350.9 0.0 copy-done
  350.9 1.7 copy.23
  (2 shorter events, 0.0 us)
Async XLA Ops:
  325.7 17.1 %slice-start.3 = ((s8[9437184]{0:T(1024)(128)(4,1)}), s8[4194304]{0:T(1024)(128)(4,1)S(1)}, s32[]{:S(2)}) async-start(s8[9437184]{0:T(1024)(128)(4,1)} %bitcast.2), calls=%async_computation.3 | async-start | bytes 8388608
  325.8 17.1 %slice-start.4 = ((s8[9437184]{0:T(1024)(128)(4,1)}), s8[4194304]{0:T(1024)(128)(4,1)S(1)}, s32[]{:S(2)}) async-start(s8[9437184]{0:T(1024)(128)(4,1)} %bitcast.2), calls=%async_computation.4 | async-start | bytes 8388608
  334.1 8.8 %slice-start.5 = ((s8[9437184]{0:T(1024)(128)(4,1)}), s8[1048576]{0:T(1024)(128)(4,1)S(1)}, s32[]{:S(2)}) async-start(s8[9437184]{0:T(1024)(128)(4,1)} %bitcast.2), calls=%async_computation.5 | async-start | bytes 2097152
  334.1 12.5 %slice-start = ((s8[9437184]{0:T(1024)(128)(4,1)}), s8[4194304]{0:T(1024)(128)(4,1)S(1)}, s32[]{:S(2)}) async-start(s8[9437184]{0:T(1024)(128)(4,1)} %bitcast), calls=%async_computation | async-start | bytes 8388608
  334.1 12.5 %slice-start.1 = ((s8[9437184]{0:T(1024)(128)(4,1)}), s8[4194304]{0:T(1024)(128)(4,1)S(1)}, s32[]{:S(2)}) async-start(s8[9437184]{0:T(1024)(128)(4,1)} %bitcast), calls=%async_computation.1 | async-start | bytes 8388608
  342.9 3.8 %slice-start.2 = ((s8[9437184]{0:T(1024)(128)(4,1)}), s8[1048576]{0:T(1024)(128)(4,1)S(1)}, s32[]{:S(2)}) async-start(s8[9437184]{0:T(1024)(128)(4,1)} %bitcast), calls=%async_computation.2 | async-start | bytes 2097152
  346.7 4.3 %copy-start = (bf16[2048,768]{1,0:T(8,128)(2,1)S(1)}, bf16[2048,768]{1,0:T(8,128)(2,1)}, u32[]{:S(2)}) copy-start(bf16[2048,768]{1,0:T(8,128)(2,1)} %get-tuple-element.14) | copy-start | bytes 9437188

commit v6 on v5

--- a/solution.py
+++ b/solution.py
@@ -92,7 +92,7 @@
             device_id=peer, device_id_type=MESH)
 
     def rows_loop(count, fn):
-        block = math.gcd(count, 16)
+        block = math.gcd(count, 32)
 
         @pl.loop(0, count // block)
         def _(t):

time: 353 us -> 351 us (level)
  no operation moved by 1% of the time
where the time goes in v6:
time: 351 us
  Pallas kernels  323 us (92%)
  local copies, waits for them, and re-layouts  26.8 us (8%)
    pallas_call x1, Pallas kernels, backward_and_reduce(): pl.pallas_call(step_kernel, name='backward_and_reduce', out_shape=[jax.Sh...  323 us
    unnamed x19, local copies, waits for them, and re-layouts  26.8 us

profile of v6, /device:TPU:0, one launch (start us, length us, event | category | flops | bytes accessed | tf_op | source)
XLA Modules:
  0.0 350.8 jit_solution(8847944995378652220)
XLA Ops:
  0.6 323.3 %backward_and_reduce.1 = (f32[3072,768]{1,0:T(8,128)}, f32[768,3072]{1,0:T(8,128)}, f32[3072,768]{1,0:T(8,128)}, f32[768,3072]{1,0:T(8,128)}, bf16[2048,768]{1,0:T(8,128)(2,1)}) custom-call(bf16[2048,768]{1,0:T(8,128)(2,1)} %refs_0_.1, bf16[2048,3072]{1,0:T(8,128)(2,1)} %refs_1_.1, bf16[2048,768]{1,0:T(8,128)(2,1)} %refs_2_.1, bf16[768,3072]{1,0:T(8,128)(2,1)} %refs_3_.1, ...), custom_call_target="tpu_custom_call" | custom-call | tf_op jit(solution)/shard_map/backward_and_reduce/pallas_call | solution.py:426
  323.9 0.0 slice-start.3
  323.9 0.0 slice-start.4
  324.0 8.4 %copy.19 = f32[3072,768]{1,0:T(8,128)} copy(f32[3072,768]{1,0:T(8,128)} %get-tuple-element.10) | data formatting | bytes 18874368
  332.3 0.0 slice-start.5
  332.3 0.0 slice-start
  332.3 0.0 slice-start.1
  332.3 8.8 %copy.20 = f32[768,3072]{1,0:T(8,128)} copy(f32[768,3072]{1,0:T(8,128)} %get-tuple-element.11) | data formatting | bytes 18874368
  341.1 0.0 slice-done.3
  341.1 0.0 slice-done.4
  341.1 0.0 slice-done.5
  341.1 0.0 slice-start.2
  341.1 3.7 %copy.21 = f32[3072,768]{1,0:T(8,128)} copy(f32[3072,768]{1,0:T(8,128)S(1)} %bitcast.3) | data formatting | bytes 18874368
  344.9 0.0 slice-done
  344.9 0.0 slice-done.1
  344.9 0.0 slice-done.2
  344.9 0.0 copy-start
  344.9 4.2 %copy.22 = f32[768,3072]{1,0:T(8,128)} copy(f32[768,3072]{1,0:T(8,128)S(1)} %bitcast.1) | data formatting | bytes 18874368
  349.1 0.0 copy-done
  349.1 1.7 copy.23
  (2 shorter events, 0.0 us)
Async XLA Ops:
  323.9 17.1 %slice-start.3 = ((s8[9437184]{0:T(1024)(128)(4,1)}), s8[4194304]{0:T(1024)(128)(4,1)S(1)}, s32[]{:S(2)}) async-start(s8[9437184]{0:T(1024)(128)(4,1)} %bitcast.2), calls=%async_computation.3 | async-start | bytes 8388608
  323.9 17.1 %slice-start.4 = ((s8[9437184]{0:T(1024)(128)(4,1)}), s8[4194304]{0:T(1024)(128)(4,1)S(1)}, s32[]{:S(2)}) async-start(s8[9437184]{0:T(1024)(128)(4,1)} %bitcast.2), calls=%async_computation.4 | async-start | bytes 8388608
  332.3 8.8 %slice-start.5 = ((s8[9437184]{0:T(1024)(128)(4,1)}), s8[1048576]{0:T(1024)(128)(4,1)S(1)}, s32[]{:S(2)}) async-start(s8[9437184]{0:T(1024)(128)(4,1)} %bitcast.2), calls=%async_computation.5 | async-start | bytes 2097152
  332.3 12.5 %slice-start = ((s8[9437184]{0:T(1024)(128)(4,1)}), s8[4194304]{0:T(1024)(128)(4,1)S(1)}, s32[]{:S(2)}) async-start(s8[9437184]{0:T(1024)(128)(4,1)} %bitcast), calls=%async_computation | async-start | bytes 8388608
  332.3 12.5 %slice-start.1 = ((s8[9437184]{0:T(1024)(128)(4,1)}), s8[4194304]{0:T(1024)(128)(4,1)S(1)}, s32[]{:S(2)}) async-start(s8[9437184]{0:T(1024)(128)(4,1)} %bitcast), calls=%async_computation.1 | async-start | bytes 8388608
  341.1 3.8 %slice-start.2 = ((s8[9437184]{0:T(1024)(128)(4,1)}), s8[1048576]{0:T(1024)(128)(4,1)S(1)}, s32[]{:S(2)}) async-start(s8[9437184]{0:T(1024)(128)(4,1)} %bitcast), calls=%async_computation.2 | async-start | bytes 2097152
  344.9 4.3 %copy-start = (bf16[2048,768]{1,0:T(8,128)(2,1)S(1)}, bf16[2048,768]{1,0:T(8,128)(2,1)}, u32[]{:S(2)}) copy-start(bf16[2048,768]{1,0:T(8,128)(2,1)} %get-tuple-element.14) | copy-start | bytes 9437188
